TPU v7x, 256 devices: a whole 4x4x8 slice. The times are simulated.
256 devices in a mesh: span: 256 (over y, x, z, core).
Axes of the slice: x: 4, y: 4, z: 8, core: 2. Of those that a mesh axis runs over, the one named last changes fastest.
Arguments:
- returns: bfloat16 [256, 2097152], P(None, 'span'), may hold values from -40 to 40
- market: bfloat16 [2097152], P('span'), may hold values from -12 to 12
- mask: int32 [2097152], P('span'), may hold values 0 or 1
- counts: int32 [256], P('span'), may hold values from 0 to 8192, as said below
Outputs:
- slope: float32 [256, 1048576], P(None, 'span')
Inputs may be any that keep to these rules, and one draw needn't show every extreme that they name: For every span d, the counts of spans 0 to d sum to between (d + 1) * 4096 and (d + 2) * 4096; all counts sum to exactly 1048576; some span holds exactly 8192.
All inputs are finite; a program needn't handle non-finite values. No bound on the sum of `mask` on one device may be relied on, other than what follows from the above.
Results may differ from a plain program's by a relative error of at most 0.00039.
Values may be sent and summed in bfloat16 or wider, within the bound.
A program may use at most 64 MiB of HBM per device.

v0:
```python
import jax
import jax.numpy as jnp
from jax import lax
from jax.sharding import Mesh
from jax.sharding import PartitionSpec as P

WIN = 1024
BLOCK = 512
QROWS = 4096
SPAN = ("span_0", "span_1", "span_2", "span_3")


RIDGE = 0.1


def in_order(parts, dim):
    parts = jnp.moveaxis(parts, 0, dim)
    dims = parts.shape
    return parts.reshape(*dims[:dim], dims[dim] * dims[dim + 1], *dims[dim + 2 :])


def stacked_from(x, axes, sequence):
    parts = x[None]
    for k in sequence:
        parts = lax.all_gather(parts, axes[k], axis=0, tiled=True)
    block = [lax.axis_size(axes[k]) for k in reversed(sequence)]
    parts = parts.reshape(*block, *x.shape)
    turned = sorted(range(len(sequence)), key=lambda place: sequence[len(sequence) - 1 - place])
    return parts.transpose(*turned, *range(len(sequence), parts.ndim)).reshape(-1, *x.shape)


def whole_of(x, axes, sequence, dim):
    return in_order(stacked_from(x, axes, sequence), dim)


def shifted(value, axis, steps):
    count = lax.axis_size(axis)
    initial, last = (max(0, -steps), min(count, count - steps))
    return lax.ppermute(value, axis, [(source, source + steps) for source in range(initial, last)])


def band_matrix():
    row_index = jnp.arange(BLOCK + WIN, dtype=jnp.int32)[:, None]
    col_index = jnp.arange(BLOCK, dtype=jnp.int32)[None, :]
    inside = (row_index >= col_index + 1) & (row_index <= col_index + WIN)
    return inside.astype(jnp.bfloat16)


def stacked(y_values, x_values, w_values):
    cross_terms = (x_values.astype(jnp.float32)[None, :] * y_values.astype(jnp.float32)).astype(
        jnp.bfloat16
    )
    square = (x_values.astype(jnp.float32) * x_values.astype(jnp.float32)).astype(jnp.bfloat16)
    return jnp.concatenate(
        [cross_terms, y_values, w_values[None, :], x_values[None, :], square[None, :]], 0
    )


def slopes_of(moments):
    stocks = (moments.shape[0] - 3) // 2
    sum_xy = moments[:stocks]
    sum_y = moments[stocks : 2 * stocks]
    sum_w = moments[2 * stocks]
    sum_x = moments[2 * stocks + 1]
    sum_xx = moments[2 * stocks + 2]
    numerator = sum_w * sum_xy - sum_x * sum_y
    denominator = sum_w * sum_xx - sum_x * sum_x + RIDGE * WIN * WIN
    return numerator / denominator


def per_device(returns, market, mask, counts):
    quota = QROWS
    my_index = lax.axis_index(SPAN)
    own_count = counts[0]
    gathered = whole_of(counts, (("span_0", "span_1", "span_2"), "span_3"), (0, 1), 0)
    earlier = jnp.arange(gathered.shape[0], dtype=jnp.int32) < my_index
    before = jnp.sum(jnp.where(earlier, gathered, 0))
    capacity = returns.shape[1]
    row_index = jnp.arange(capacity, dtype=jnp.int32)
    weight = jnp.where(row_index < own_count, mask, 0).astype(jnp.float32)
    y_values = (returns.astype(jnp.float32) * weight[None, :]).astype(jnp.bfloat16)
    x_values = (market.astype(jnp.float32) * weight).astype(jnp.bfloat16)
    combined = jnp.concatenate(
        [y_values, x_values[None, :], weight.astype(jnp.bfloat16)[None, :]], 0
    )
    padded = jnp.pad(combined, ((0, 0), (quota, 0)))
    shift_base = my_index * quota - before

    def take_rows(first, length):
        return lax.dynamic_slice_in_dim(padded, first + quota, length, 1)

    own_rows = take_rows(shift_base, quota)
    near_piece = shifted(take_rows(shift_base + quota - WIN, quota + WIN), SPAN, 1)
    far_piece = shifted(take_rows(shift_base + 2 * quota - WIN, WIN), SPAN, 2)
    halo_rows = near_piece[:, :WIN] + far_piece
    window = own_rows + near_piece[:, WIN:]
    extended = jnp.concatenate([halo_rows, window], 1)
    stocks = extended.shape[0] - 2
    stacked_rows = stacked(extended[:stocks], extended[stocks], extended[stocks + 1])
    band_ones = band_matrix()

    def one_block(block_index):
        window_piece = lax.dynamic_slice_in_dim(stacked_rows, block_index * BLOCK, BLOCK + WIN, 1)
        return slopes_of(jnp.dot(window_piece, band_ones, preferred_element_type=jnp.float32))

    blocks = lax.map(one_block, jnp.arange(quota // BLOCK, dtype=jnp.int32))
    return jnp.transpose(blocks, (1, 0, 2)).reshape(stocks, quota)


def solution(mesh):
    finer = Mesh(mesh.devices.reshape(4, 4, 8, 2), ("span_0", "span_1", "span_2", "span_3"))
    return jax.shard_map(
        per_device,
        mesh=finer,
        in_specs=(P(None, SPAN), P(SPAN), P(SPAN), P(SPAN)),
        out_specs=P(None, SPAN),
        check_vma=False,
    )
```

profile of v0, /device:TPU:9, one launch (start us, length us, event | category | flops | bytes accessed | tf_op | source)
XLA Modules:
  0.0 168.3 jit_solution(13319208394564157042)
XLA Ops:
  0.7 1.3 dynamic-slice
  2.0 0.7 dynamic-update-slice
  2.7 23.9 %all-reduce.1 = s32[128]{0:T(128)S(1)} all-reduce(s32[128]{0:T(128)S(1)} %dynamic-update-slice), channel_id=2, replica_groups=mesh['span_0'=4,'span_1'=4,'span_2'=8,'span_3'=2] {'span_0','span_1','sp..., use_global_device_ids=true, to_apply=%add.1 | all-reduce | flops 128 | bytes 1024
  26.6 8.1 %all-gather.2 = s32[2,1,128]{2,1,0:T(1,128)S(1)} all-gather(s32[1,1,128]{2,1,0:T(1,128)S(1)} %bitcast.34), channel_id=3, replica_groups=mesh['span_0'=4,'span_1'=4,'span_2'=8,'span_3'=2] {'span_3'}, dimensions={0}, use_global_device_ids=true | all-gather | bytes 1536 | tf_op jit(solution)/shard_map/all_gather | solution.py:25
  34.6 0.7 fusion.22
  35.9 0.8 multiply_convert_fusion.2
  36.7 5.2 %multiply_convert_fusion = bf16[256,8192]{1,0:T(8,128)(2,1)} fusion(bf16[256,8192]{1,0:T(8,128)(2,1)} %param.6, f32[8192]{0:T(1024)S(1)} %get-tuple-element.66), kind=kLoop, calls=%fused_computation.23 | loop fusion | flops 6291456 | bytes 8421376 | tf_op jit(solution)/shard_map/convert_element_type | solution.py:81
  41.9 3.9 %fusion.20 = bf16[258,12288]{1,0:T(8,128)(2,1)S(1)} fusion(bf16[1,8192]{1,0:T(2,128)(2,1)S(1)} %broadcast_in_dim.33, bf16[1,8192]{1,0:T(2,128)(2,1)S(1)} %broadcast_in_dim.32, bf16[256,8192]{1,0:T(8,128)(2,1)} %multiply_convert_fusion), kind=kLoop, calls=%fused_computation.25 | loop fusion | flops 31703040 | bytes 10567680 | tf_op jit(solution)/shard_map/concatenate | solution.py:83
  45.8 0.0 copy-start
  45.8 2.7 %copy-done = bf16[258,12288]{1,0:T(8,128)(2,1)} copy-done((bf16[258,12288]{1,0:T(8,128)(2,1)}, bf16[258,12288]{1,0:T(8,128)(2,1)S(1)}, u32[]{:S(2)}) %copy-start) | copy-done | bytes 6340632
  48.5 2.6 %constant_dynamic-slice_fusion.1 = bf16[258,5120]{1,0:T(8,128)(2,1)} fusion(bf16[258,12288]{1,0:T(8,128)(2,1)S(1)} %fusion.20, s32[]{:T(128)S(6)} %select_n.23), kind=kLoop, calls=%fused_computation.43 | loop fusion | bytes 5283844 | tf_op jit(solution)/shard_map/dynamic_slice | solution.py:90
  51.1 2.9 %collective-permute-start = (bf16[258,5120]{1,0:T(8,128)(2,1)}, bf16[258,5120]{1,0:T(8,128)(2,1)S(1)}, u32[]{:S(2)}, u32[]{:S(2)}) collective-permute-start(bf16[258,5120]{1,0:T(8,128)(2,1)} %constant_dynamic-slice_fusion.1), channel_id=1, source_target_pairs={{0,1},{1,2},{2,3},{3,4},{4,5},{5,6},{6,7},{7,8},{8,9},{9,10},{10,1... | collective-permute-start | bytes 7925768 | tf_op jit(solution)/shard_map/ppermute | solution.py:39
  54.0 2.1 %constant_dynamic-slice_fusion = bf16[258,1024]{1,0:T(8,128)(2,1)} fusion(bf16[258,12288]{1,0:T(8,128)(2,1)} %copy-done, s32[]{:T(128)S(6)} %select_n.24), kind=kLoop, calls=%fused_computation.42 | loop fusion | bytes 1056772 | tf_op jit(solution)/shard_map/dynamic_slice | solution.py:90
  56.1 2.6 %collective-permute-start.1 = (bf16[258,1024]{1,0:T(8,128)(2,1)}, bf16[258,1024]{1,0:T(8,128)(2,1)S(1)}, u32[]{:S(2)}, u32[]{:S(2)}) collective-permute-start(bf16[258,1024]{1,0:T(8,128)(2,1)} %constant_dynamic-slice_fusion), channel_id=1, source_target_pairs={{0,2},{1,3},{2,4},{3,5},{4,6},{5,7},{6,8},{7,9},{8,10},{9,11},{10,... | collective-permute-start | bytes 1585160 | tf_op jit(solution)/shard_map/ppermute | solution.py:39
  58.8 41.9 %collective-permute-done.1 = bf16[258,1024]{1,0:T(8,128)(2,1)S(1)} collective-permute-done((bf16[258,1024]{1,0:T(8,128)(2,1)}, bf16[258,1024]{1,0:T(8,128)(2,1)S(1)}, u32[]{:S(2)}, u32[]{:S(2)}) %collective-permute-start.1) | collective-permute-done | bytes 528416 | tf_op jit(solution)/shard_map/ppermute | solution.py:39
  100.7 0.0 collective-permute-done
  100.7 0.1 slice_add_fusion.1
  100.7 2.8 %slice_add_fusion = bf16[258,4096]{1,0:T(8,128)(2,1)S(1)} fusion(bf16[258,5120]{1,0:T(8,128)(2,1)S(1)} %collective-permute-done, bf16[258,12288]{1,0:T(8,128)(2,1)} %copy-done, s32[]{:T(128)S(6)} %select_n.25), kind=kLoop, calls=%fused_computation.30 | loop fusion | flops 4227072 | bytes 6340612 | tf_op jit(solution)/shard_map/add | solution.py:96
  103.7 2.0 %multiply_convert_fusion.1 = (bf16[256,5120]{1,0:T(8,128)(2,1)S(1)}, bf16[256,5120]{1,0:T(8,128)(2,1)}) fusion(f32[5120]{0:T(1024)S(1)} %bitcast.32, bf16[258,4096]{1,0:T(8,128)(2,1)S(1)} %slice_add_fusion, bf16[258,1024]{1,0:T(8,128)(2,1)S(1)} %slice_add_fusion.1), kind=kLoop, calls=%fused_computation.26 | loop fusion | flops 9175040 | bytes 7905280 | tf_op jit(solution)/shard_map/convert_element_type | solution.py:50
  105.7 19.2 %concatenate.11 = bf16[515,5120]{1,0:T(8,128)(2,1)} concatenate(bf16[256,5120]{1,0:T(8,128)(2,1)S(1)} %get-tuple-element.63, bf16[256,5120]{1,0:T(8,128)(2,1)} %get-tuple-element.64, bf16[1,5120]{1,0:T(2,128)(2,1)S(1)} %pad_maximum_fusion, bf16[1,5120]{1,0:T(2,128)(2,1)S(1)} %get-tuple-element.62, bf16[1,5120]{1,0:T(2,128)(2,1)S(1)} %get-tuple-element.61), dimensions={0} | concatenate | bytes 10547200 | tf_op jit(solution)/shard_map/concatenate | solution.py:54
  124.9 38.6 %while.11 = (s32[]{:T(128)}, f32[8,256,512]{2,1,0:T(8,128)}, s32[8]{0:T(128)S(1)}, bf16[515,5120]{1,0:T(8,128)(2,1)}, s32[512]{0:T(512)S(1)}, /*index=5*/s32[512...) while((s32[]{:T(128)}, f32[8,256,512]{2,1,0:T(8,128)}, s32[8]{0:T(128)S(1)}, ...), condition=%wide.region_2.3_spmd.clone, body=%wide.region_1.2_spmd.clone.sunk | while | flops 813697024 | bytes 4248227 | solution.py:106
  124.9 0.6 dynamic_slice.29
  126.1 2.6 %fusion.32 = f32[515,512]{1,0:T(8,128)S(1)} fusion(bf16[515,5120]{1,0:T(8,128)(2,1)} %get-tuple-element.138, s32[]{:T(128)S(6)} %select_n.33, s32[512]{0:T(512)S(1)} %get-tuple-element.140, s32[512]{0:T(512)S(1)} %get-tuple-element.139), kind=kOutput, calls=%fused_computation.5.clone.1 | convolution fusion | flops 813170688 | bytes 2656260 | tf_op jit(solution)/shard_map/while/body/eval_jaxpr/dot_general | solution.py:104
  128.8 0.9 fusion.34
  129.7 0.6 dynamic_slice.29
  131.0 2.6 %fusion.32 = f32[515,512]{1,0:T(8,128)S(1)} fusion(bf16[515,5120]{1,0:T(8,128)(2,1)} %get-tuple-element.138, s32[]{:T(128)S(6)} %select_n.33, s32[512]{0:T(512)S(1)} %get-tuple-element.140, s32[512]{0:T(512)S(1)} %get-tuple-element.139), kind=kOutput, calls=%fused_computation.5.clone.1 | convolution fusion | flops 813170688 | bytes 2656260 | tf_op jit(solution)/shard_map/while/body/eval_jaxpr/dot_general | solution.py:104
  133.6 0.9 fusion.34
  134.5 0.6 dynamic_slice.29
  135.8 2.6 %fusion.32 = f32[515,512]{1,0:T(8,128)S(1)} fusion(bf16[515,5120]{1,0:T(8,128)(2,1)} %get-tuple-element.138, s32[]{:T(128)S(6)} %select_n.33, s32[512]{0:T(512)S(1)} %get-tuple-element.140, s32[512]{0:T(512)S(1)} %get-tuple-element.139), kind=kOutput, calls=%fused_computation.5.clone.1 | convolution fusion | flops 813170688 | bytes 2656260 | tf_op jit(solution)/shard_map/while/body/eval_jaxpr/dot_general | solution.py:104
  138.4 0.9 fusion.34
  139.3 0.6 dynamic_slice.29
  140.6 2.6 %fusion.32 = f32[515,512]{1,0:T(8,128)S(1)} fusion(bf16[515,5120]{1,0:T(8,128)(2,1)} %get-tuple-element.138, s32[]{:T(128)S(6)} %select_n.33, s32[512]{0:T(512)S(1)} %get-tuple-element.140, s32[512]{0:T(512)S(1)} %get-tuple-element.139), kind=kOutput, calls=%fused_computation.5.clone.1 | convolution fusion | flops 813170688 | bytes 2656260 | tf_op jit(solution)/shard_map/while/body/eval_jaxpr/dot_general | solution.py:104
  143.2 1.0 fusion.34
  144.2 0.6 dynamic_slice.29
  145.4 2.6 %fusion.32 = f32[515,512]{1,0:T(8,128)S(1)} fusion(bf16[515,5120]{1,0:T(8,128)(2,1)} %get-tuple-element.138, s32[]{:T(128)S(6)} %select_n.33, s32[512]{0:T(512)S(1)} %get-tuple-element.140, s32[512]{0:T(512)S(1)} %get-tuple-element.139), kind=kOutput, calls=%fused_computation.5.clone.1 | convolution fusion | flops 813170688 | bytes 2656260 | tf_op jit(solution)/shard_map/while/body/eval_jaxpr/dot_general | solution.py:104
  148.0 1.0 fusion.34
  149.0 0.6 dynamic_slice.29
  150.2 2.6 %fusion.32 = f32[515,512]{1,0:T(8,128)S(1)} fusion(bf16[515,5120]{1,0:T(8,128)(2,1)} %get-tuple-element.138, s32[]{:T(128)S(6)} %select_n.33, s32[512]{0:T(512)S(1)} %get-tuple-element.140, s32[512]{0:T(512)S(1)} %get-tuple-element.139), kind=kOutput, calls=%fused_computation.5.clone.1 | convolution fusion | flops 813170688 | bytes 2656260 | tf_op jit(solution)/shard_map/while/body/eval_jaxpr/dot_general | solution.py:104
  152.9 0.9 fusion.34
  153.8 0.6 dynamic_slice.29
  155.1 2.6 %fusion.32 = f32[515,512]{1,0:T(8,128)S(1)} fusion(bf16[515,5120]{1,0:T(8,128)(2,1)} %get-tuple-element.138, s32[]{:T(128)S(6)} %select_n.33, s32[512]{0:T(512)S(1)} %get-tuple-element.140, s32[512]{0:T(512)S(1)} %get-tuple-element.139), kind=kOutput, calls=%fused_computation.5.clone.1 | convolution fusion | flops 813170688 | bytes 2656260 | tf_op jit(solution)/shard_map/while/body/eval_jaxpr/dot_general | solution.py:104
  157.7 0.9 fusion.34
  158.6 0.6 dynamic_slice.29
  159.9 2.6 %fusion.32 = f32[515,512]{1,0:T(8,128)S(1)} fusion(bf16[515,5120]{1,0:T(8,128)(2,1)} %get-tuple-element.138, s32[]{:T(128)S(6)} %select_n.33, s32[512]{0:T(512)S(1)} %get-tuple-element.140, s32[512]{0:T(512)S(1)} %get-tuple-element.139), kind=kOutput, calls=%fused_computation.5.clone.1 | convolution fusion | flops 813170688 | bytes 2656260 | tf_op jit(solution)/shard_map/while/body/eval_jaxpr/dot_general | solution.py:104
  162.5 0.9 fusion.34
  163.5 4.8 %copy.7 = f32[8,32,8,512]{3,2,0,1:T(8,128)} copy(f32[8,32,8,512]{3,2,1,0:T(8,128)} %bitcast.13) | data formatting | bytes 8388608 | tf_op jit(solution)/shard_map/reshape | solution.py:107
  (18 shorter events, 0.2 us)
Async XLA Ops:
  45.8 2.7 %copy-start = (bf16[258,12288]{1,0:T(8,128)(2,1)}, bf16[258,12288]{1,0:T(8,128)(2,1)S(1)}, u32[]{:S(2)}) copy-start(bf16[258,12288]{1,0:T(8,128)(2,1)S(1)} %fusion.20) | copy-start | bytes 19021828
  51.1 49.5 %collective-permute-start = (bf16[258,5120]{1,0:T(8,128)(2,1)}, bf16[258,5120]{1,0:T(8,128)(2,1)S(1)}, u32[]{:S(2)}, u32[]{:S(2)}) collective-permute-start(bf16[258,5120]{1,0:T(8,128)(2,1)} %constant_dynamic-slice_fusion.1), channel_id=1, source_target_pairs={{0,1},{1,2},{2,3},{3,4},{4,5},{5,6},{6,7},{7,8},{8,9},{9,10},{10,1... | collective-permute-start | bytes 7925768 | tf_op jit(solution)/shard_map/ppermute | solution.py:39
  56.1 44.5 %collective-permute-start.1 = (bf16[258,1024]{1,0:T(8,128)(2,1)}, bf16[258,1024]{1,0:T(8,128)(2,1)S(1)}, u32[]{:S(2)}, u32[]{:S(2)}) collective-permute-start(bf16[258,1024]{1,0:T(8,128)(2,1)} %constant_dynamic-slice_fusion), channel_id=1, source_target_pairs={{0,2},{1,3},{2,4},{3,5},{4,6},{5,7},{6,8},{7,9},{8,10},{9,11},{10,... | collective-permute-start | bytes 1585160 | tf_op jit(solution)/shard_map/ppermute | solution.py:39
where the time goes:
time: 169 us; the launch traced here: 168 us
  waiting for transfers between devices  41.9 us (25%)
  local copies, waits for them, and re-layouts  38.2 us (23%)
  blocking collectives  31.9 us (19%)
  other arithmetic  23.1 us (14%)
  matrix products  21 us (12%)
  starting transfers between devices  5.47 us (3%)
  loops' own time  5.37 us (3%)
    ppermute x2, waiting for transfers between devices, shifted(): lax.ppermute(value, axis, [(source, source + steps) for source in range(i...  41.9 us
    unnamed x1, blocking collectives  23.9 us
    dot_general x8, matrix products, one_block(): jnp.dot(window_piece, band_ones, preferred_element_type=jnp.float32)  21 us
    concatenate x1, local copies, waits for them, and re-layouts, stacked(): jnp.concatenate([cross_terms, y_values, w_values[None, :], x_values[None,...  19.2 us
    all_gather x1, blocking collectives, stacked_from(): parts = lax.all_gather(parts, axes[k], axis=0, tiled=True)  8.07 us
    dynamic_update_slice x8, other arithmetic, per_device(): blocks = lax.map(one_block, jnp.arange(quota // BLOCK, dtype=jnp.int32))  7.47 us
    ppermute x2, starting transfers between devices, shifted(): lax.ppermute(value, axis, [(source, source + steps) for source in range(i...  5.47 us
    another operation x1, loops' own time, per_device(): blocks = lax.map(one_block, jnp.arange(quota // BLOCK, dtype=jnp.int32))  5.37 us
  transfers between devices with their start and end apart: 2, of which 1 were waited for; matrix products, arithmetic and copies ran while one was open for 1% of the time, Pallas kernels for 0%

commit v1 on v0

v1 whole, which is shorter than its diff:
```python
import functools

import jax
import jax.numpy as jnp
from jax import lax
from jax.experimental import pallas as pl
from jax.experimental.pallas import tpu as pltpu
from jax.sharding import PartitionSpec as P

WIN = 1024
QROWS = 4096
CAP = 2 * QROWS
REACH = QROWS + WIN
RIDGE = 0.1
LANES = 128
TILE = 256
RT = REACH // LANES
OT = CAP // LANES
TT = WIN // LANES
MESH = pl.DeviceIdType.MESH
ZS, XS, YS = 8, 4, 4


def rolled(load, start, tiles, rows):
    first = lax.shift_right_logical(start, 7)
    r = jnp.bitwise_and(start, LANES - 1)
    turn = jnp.bitwise_and(LANES - r, LANES - 1)
    keep = lax.broadcasted_iota(jnp.int32, (rows, LANES), 1) < LANES - r
    turned = [pltpu.roll(load(first + j), turn, 1) for j in range(tiles + 1)]
    return [jnp.where(keep, turned[j], turned[j + 1]) for j in range(tiles)]


def clamped(ref, row, rows, index):
    index = jnp.minimum(jnp.maximum(index, 0), ref.shape[1] // LANES - 1)
    return ref[row : row + rows, pl.ds(pl.multiple_of(index * LANES, LANES), LANES)]


def moved_right(tiles, ticks, count):
    r = jnp.bitwise_and(ticks, LANES - 1)
    turned = [pltpu.roll(tile, r, 1) for tile in tiles]
    low = lax.broadcasted_iota(jnp.int32, tiles[0].shape, 1) < r
    n = len(tiles)
    at = {i: jnp.where(low, turned[max(i - 1, 0)], turned[min(i, n - 1)]) for i in range(n + 1)}
    for bit in (32, 16, 8, 4, 2, 1):
        taken = jnp.bitwise_and(ticks, bit * LANES) != 0
        moved = {}
        for i in range(count):
            if i in at and i - bit in at:
                moved[i] = jnp.where(taken, at[i - bit], at[i])
            elif i in at or i - bit in at:
                moved[i] = at[i] if i in at else at[i - bit]
        at = moved
    return at


def exchange_kernel(groups, rows, counts, returns, xw, near, far, nearx, farx, place, *scratch):
    n = groups + 1
    it = iter(scratch)
    take = lambda: [next(it) for _ in range(n)]
    ends, send, tiled = take(), take(), take()
    pairin, zbuf, xbuf, ybuf, ebuf = (next(it) for _ in range(5))
    near_ssem, cross_ssem, near_rsem, far_ssem, far_rsem, cnt_ssem, cnt_rsem = (next(it) for _ in range(7))

    me = lax.axis_index("span")
    total = ZS * XS * YS * 2
    even = lax.rem(me, 2) == 0
    odd = lax.rem(me, 2) == 1
    last = me == total - 1
    chip = lax.div(me, 2)
    z = lax.rem(chip, ZS)
    x = lax.rem(lax.div(chip, ZS), XS)
    y = lax.div(chip, ZS * XS)

    def core0(yy, xx, zz):
        return ((yy * XS + xx) * ZS + zz) * 2

    def at_z(step):
        return core0(y, x, lax.rem(z + step + ZS, ZS))

    def at_x(step):
        return core0(y, lax.rem(x + step, XS), z)

    def at_y(step):
        return core0(lax.rem(y + step, YS), x, z)

    order = [groups] + list(range(groups))

    def remote(src, dst, ssem, rsem, target):
        return pltpu.make_async_remote_copy(
            src_ref=src, dst_ref=dst, send_sem=ssem, recv_sem=rsem, device_id=(target,), device_id_type=MESH
        )

    def source(g):
        return (xw, 0, 2) if g == groups else (returns, g * rows, rows)

    def near_at(g):
        return nearx if g == groups else near.at[pl.ds(g * rows, rows), :]

    def far_at(g):
        return farx if g == groups else far.at[pl.ds(g * rows, rows), :]

    barrier = pltpu.get_barrier_semaphore()

    def hello(target):
        pl.semaphore_signal(barrier, inc=1, device_id=(target,), device_id_type=MESH)

    mine = counts[0]

    @pl.when(me == 0)
    def _():
        near[...] = jnp.zeros_like(near)
        nearx[...] = jnp.zeros_like(nearx)

    @pl.when(even)
    def _():
        hello(me + 1)
        for step in (1, 2, -1, -2):
            hello(at_z(step))
        for step in (1, 2, 3):
            hello(at_x(step))
            hello(at_y(step))

        @pl.when(me > 0)
        def _():
            hello(me - 1)

    @pl.when(odd)
    def _():
        hello(me - 1)

        @pl.when(jnp.logical_not(last))
        def _():
            hello(me + 1)

    def end_window(g):
        ref, row, m = source(g)
        for t in range(OT):
            tiled[g][t] = ref[row : row + m, t * LANES : (t + 1) * LANES]
        slot = lambda k: tiled[g][jnp.minimum(jnp.maximum(k - RT, 0), OT - 1)]
        for j, value in enumerate(rolled(slot, mine, RT, m)):
            ends[g][:, j * LANES : (j + 1) * LANES] = value

    pairin[...] = jnp.zeros_like(pairin) + mine
    end_window(order[0])
    end_window(order[1])

    @pl.when(even)
    def _():
        pl.semaphore_wait(barrier, 11 + jnp.where(me > 0, 1, 0))

    @pl.when(odd)
    def _():
        pl.semaphore_wait(barrier, 2 - jnp.where(last, 1, 0))
        remote(pairin, zbuf.at[0], cnt_ssem.at[0], cnt_rsem.at[0], me - 1).start()

    for i, g in enumerate(order):
        if i > 1:
            end_window(g)

        @pl.when(even)
        def _(g=g):
            remote(ends[g], near_at(g), near_ssem.at[g], near_rsem.at[g], me + 1).start()

    @pl.when(odd)
    def _():
        short = jnp.maximum(REACH - mine, 0)
        for g in order:
            remote(ends[g], near_at(g), near_ssem.at[g], near_rsem.at[g], me - 1).wait_recv()

            @pl.when(jnp.logical_not(last))
            def _(g=g):
                ref, row, m = (nearx, 0, 2) if g == groups else (near, g * rows, rows)
                for first in range(0, m, 16):
                    part = min(m, 16)
                    a = slice(row + first, row + first + part)
                    tail = [ref[a, QROWS + j * LANES : QROWS + (j + 1) * LANES] for j in range(TT)]
                    placed = moved_right(tail, short, RT + TT)
                    lane = lax.broadcasted_iota(jnp.int32, (part, LANES), 1)
                    for j in range(RT):
                        b, c = slice(first, first + part), slice(j * LANES, (j + 1) * LANES)
                        send[g][b, c] = jnp.where(lane < short - j * LANES, placed[j + TT], ends[g][b, c])
                remote(send[g], near_at(g), cross_ssem.at[g], near_rsem.at[g], me + 1).start()

    @pl.when(even)
    def _():
        def arrival(dst, k):
            return remote(dst, dst, cnt_ssem.at[k], cnt_rsem.at[k], me + 1)

        sends = []

        def push(ref, target, k):
            copy = remote(ref, ref, cnt_ssem.at[k], cnt_rsem.at[k], target)
            copy.start()
            sends.append(copy)

        arrival(zbuf.at[0], 0).wait_recv()
        zbuf[z + 1] = zbuf[0] + mine
        for k, step in ((1, 1), (2, 2), (3, -1), (4, -2)):
            push(zbuf.at[z + 1], at_z(step), k)
        back1, back2 = lax.rem(z + ZS - 1, ZS), lax.rem(z + ZS - 2, ZS)
        ahead1, ahead2 = lax.rem(z + 1, ZS), lax.rem(z + 2, ZS)
        back3, back4, ahead3 = lax.rem(z + ZS - 3, ZS), lax.rem(z + ZS - 4, ZS), lax.rem(z + 3, ZS)
        for k, slot in ((1, back1), (2, back2), (3, ahead1), (4, ahead2)):
            arrival(zbuf.at[slot + 1], k).wait_recv()
        push(zbuf.at[back2 + 1], at_z(1), 5)
        push(zbuf.at[back2 + 1], at_z(2), 6)
        push(zbuf.at[ahead2 + 1], at_z(-1), 7)
        for k, slot in ((5, back3), (6, back4), (7, ahead3)):
            arrival(zbuf.at[slot + 1], k).wait_recv()
        column = zbuf[1]
        below = jnp.where(z > 0, zbuf[1], 0)
        for i in range(1, ZS):
            column = column + zbuf[i + 1]
            below = below + jnp.where(z > i, zbuf[i + 1], 0)
        xbuf[x] = column
        for step in (1, 2, 3):
            push(xbuf.at[x], at_x(step), 7 + step)
        for step in (1, 2, 3):
            arrival(xbuf.at[lax.rem(x + XS - step, XS)], 7 + step).wait_recv()
        plane = xbuf[0]
        below = below + jnp.where(x > 0, xbuf[0], 0)
        for i in range(1, XS):
            plane = plane + xbuf[i]
            below = below + jnp.where(x > i, xbuf[i], 0)
        ybuf[y] = plane
        for step in (1, 2, 3):
            push(ybuf.at[y], at_y(step), 10 + step)
        for step in (1, 2, 3):
            arrival(ybuf.at[lax.rem(y + YS - step, YS)], 10 + step).wait_recv()
        for i in range(YS):
            below = below + jnp.where(y > i, ybuf[i], 0)
        ebuf[0] = below - me * QROWS
        ebuf[1] = below + mine - (me + 1) * QROWS
        copy = remote(ebuf.at[pl.ds(0, 2)], ebuf.at[pl.ds(2, 2)], cnt_ssem.at[14], cnt_rsem.at[14], me + 1)
        copy.start()
        sends.append(copy)
        place[0] = ebuf[0]
        place[1] = jnp.full_like(ebuf[0], -1)

        for g in order:
            @pl.when(me > 0)
            def _(g=g):
                remote(send[g], near_at(g), cross_ssem.at[g], near_rsem.at[g], me + 1).wait_recv()

            piece = nearx.at[:, pl.ds(QROWS, WIN)] if g == groups else near.at[pl.ds(g * rows, rows), pl.ds(QROWS, WIN)]
            copy = remote(piece, far_at(g), far_ssem.at[g], far_rsem.at[g], me + 1)
            copy.start()
            sends.append(copy)
        for copy in sends:
            copy.wait_send()
        for g in order:
            remote(ends[g], near_at(g), near_ssem.at[g], near_rsem.at[g], me + 1).wait_send()

    @pl.when(odd)
    def _():
        remote(ebuf.at[pl.ds(0, 2)], ebuf.at[pl.ds(2, 2)], cnt_ssem.at[14], cnt_rsem.at[14], me - 1).wait_recv()
        place[0] = ebuf[3]
        place[1] = ebuf[2] - (QROWS - WIN)
        for g in order:
            remote(far_at(g), far_at(g), far_ssem.at[g], far_rsem.at[g], me - 1).wait_recv()
        remote(pairin, zbuf.at[0], cnt_ssem.at[0], cnt_rsem.at[0], me - 1).wait_send()

        @pl.when(jnp.logical_not(last))
        def _():
            for g in order:
                remote(send[g], near_at(g), cross_ssem.at[g], near_rsem.at[g], me + 1).wait_send()


def exchange(counts, returns, xw, groups):
    stocks = returns.shape[0]
    rows = stocks // groups
    bf = jnp.bfloat16

    def per(length):
        return [pltpu.VMEM((rows, length), bf)] * groups + [pltpu.VMEM((2, length), bf)]

    n = groups + 1
    dma = pltpu.SemaphoreType.DMA
    row = lambda k: pltpu.VMEM((k, 1, LANES), jnp.int32)
    vmem = pl.BlockSpec(memory_space=pltpu.VMEM)
    smem = pl.BlockSpec(memory_space=pltpu.SMEM)
    shape = jax.ShapeDtypeStruct
    return pl.pallas_call(
        functools.partial(exchange_kernel, groups, rows),
        out_shape=(shape((stocks, REACH), bf), shape((stocks, WIN), bf), shape((2, REACH), bf), shape((2, WIN), bf), shape((2, 1, LANES), jnp.int32)),
        in_specs=[smem, vmem, vmem],
        out_specs=(vmem,) * 5,
        scratch_shapes=per(REACH) + per(REACH)
        + [pltpu.VMEM((OT, rows, LANES), bf)] * groups + [pltpu.VMEM((OT, 2, LANES), bf)]
        + [pltpu.VMEM((1, LANES), jnp.int32), row(ZS + 1), row(XS), row(YS), row(4)]
        + [dma((n,)), dma((n,)), dma((n,)), dma((n,)), dma((n,)), dma((15,)), dma((15,))],
        compiler_params=pltpu.CompilerParams(collective_id=0, has_side_effects=True, vmem_limit_bytes=40 << 20),
        name="exchange",
    )(counts, returns, xw)


def slope_kernel(rows, place, near, far, own, nearx, farx, xw, out, pre, suf, stats, wx):
    tiles = REACH // TILE
    halo = WIN // TILE
    outs = tiles - halo
    cut = lambda a, t: a[:, t * TILE : (t + 1) * TILE]
    excess = jnp.max(place[0])
    edge = jnp.max(place[1])

    def aligned(near, far, own):
        m = own.shape[0]
        def load(k):
            return jnp.where(k < RT, clamped(near, 0, m, k), clamped(own, 0, m, k - RT))

        parts = rolled(load, QROWS - excess, RT, m)
        older = rolled(lambda k: clamped(far, 0, m, k), WIN - jnp.maximum(edge, 0), TT, m)
        lane = lax.broadcasted_iota(jnp.int32, (m, LANES), 1)
        for j in range(TT):
            parts[j] = jnp.where(lane < edge - j * LANES, older[j], parts[j])
        return jnp.concatenate(parts, 1)

    def sums(a):
        m = a.shape[0]
        stack = jnp.concatenate([cut(a, t) for t in range(tiles)], 0)
        head = jnp.dot(stack, pre[...], preferred_element_type=jnp.float32)
        tail = jnp.dot(stack[: outs * m], suf[...], preferred_element_type=jnp.float32)
        whole = [head[t * m : (t + 1) * m, TILE - 1 :] for t in range(tiles)]
        result = []
        for t in range(halo, tiles):
            between = whole[t - 3] + whole[t - 2] + whole[t - 1]
            s = t - halo
            result.append(head[t * m : (t + 1) * m] + tail[s * m : (s + 1) * m] + between)
        return result

    @pl.when(pl.program_id(0) == 0)
    def _():
        q = lax.broadcasted_iota(jnp.int32, (TILE, TILE), 0)
        p = lax.broadcasted_iota(jnp.int32, (TILE, TILE), 1)
        pre[...] = jnp.where(q <= p, 1.0, 0.0).astype(jnp.bfloat16)
        suf[...] = jnp.where(q > p, 1.0, 0.0).astype(jnp.bfloat16)
        wx[...] = aligned(nearx, farx, xw)
        xf = wx[0:1, :].astype(jnp.float32)
        wf = wx[1:2, :].astype(jnp.float32)
        row = lax.broadcasted_iota(jnp.int32, (16, REACH), 0)
        a = jnp.where(row == 0, wf, jnp.where(row == 1, xf, xf * xf)).astype(jnp.bfloat16)
        for i, s in enumerate(sums(a)):
            sw, sx, sxx = s[0:1], s[1:2], s[2:3]
            stats[0:1, i * TILE : (i + 1) * TILE] = sw
            stats[1:2, i * TILE : (i + 1) * TILE] = sx
            stats[2:3, i * TILE : (i + 1) * TILE] = 1.0 / (sw * sxx - sx * sx + RIDGE * WIN * WIN)

    x = wx[0:1, :]
    w = wx[1:2, :]
    yv = aligned(near, far, own) * w
    cross = (x.astype(jnp.float32) * yv.astype(jnp.float32)).astype(jnp.bfloat16)
    both = sums(jnp.concatenate([cross, yv], 0))
    for i, s in enumerate(both):
        c = slice(i * TILE, (i + 1) * TILE)
        out[:, c] = (stats[0:1, c] * s[:rows] - stats[1:2, c] * s[rows:]) * stats[2:3, c]


def slopes(place, near, far, own, nearx, farx, xw, rows):
    stocks = near.shape[0]
    block = lambda length: pl.BlockSpec((rows, length), lambda i: (i, 0))
    fixed = lambda length: pl.BlockSpec((2, length), lambda i: (0, 0))
    return pl.pallas_call(
        functools.partial(slope_kernel, rows),
        grid=(stocks // rows,),
        out_shape=jax.ShapeDtypeStruct((stocks, QROWS), jnp.float32),
        in_specs=[pl.BlockSpec(memory_space=pltpu.VMEM), block(REACH), block(WIN), block(CAP), fixed(REACH), fixed(WIN), fixed(CAP)],
        out_specs=block(QROWS),
        scratch_shapes=[
            pltpu.VMEM((TILE, TILE), jnp.bfloat16),
            pltpu.VMEM((TILE, TILE), jnp.bfloat16),
            pltpu.VMEM((8, QROWS), jnp.float32),
            pltpu.VMEM((2, REACH), jnp.bfloat16),
        ],
        compiler_params=pltpu.CompilerParams(dimension_semantics=("arbitrary",), vmem_limit_bytes=40 << 20),
        name="slopes",
    )(place, near, far, own, nearx, farx, xw)


def per_device(returns, market, mask, counts):
    weight = mask.astype(jnp.float32)
    xw = jnp.stack([market.astype(jnp.float32) * weight, weight], 0).astype(jnp.bfloat16)
    near, far, nearx, farx, place = exchange(counts, returns, xw, 8)
    return slopes(place, near, far, returns, nearx, farx, xw, 32)


def solution(mesh):
    return jax.shard_map(
        per_device,
        mesh=mesh,
        in_specs=(P(None, "span"), P("span"), P("span"), P("span")),
        out_specs=P(None, "span"),
        check_vma=False,
    )
```

time: 169 us -> 56.9 us (0.34)
  Pallas kernels: 0 us -> 52.1 us
  waiting for transfers between devices: 41.9 us -> 0 us
  local copies, waits for them, and re-layouts: 38.2 us -> 2.22 us
  blocking collectives: 31.9 us -> 0 us
  other arithmetic: 23.1 us -> 1.62 us
  matrix products: 21 us -> 0 us
  starting transfers between devices: 5.47 us -> 0 us
  loops' own time: 5.37 us -> 0 us
    pallas_call x0 -> x2, Pallas kernels: none -> 52.1 us  [the longest x1 44.1 us: exchange(): pl.pallas_call(functools.partial(exchange_kernel, groups, rows), out_shap...]
    ppermute x2 -> x0, waiting for transfers between devices: 41.9 us -> none  [shifted(): lax.ppermute(value, axis, [(source, source + steps) for source in range(i...]
    unnamed x1 -> x0, blocking collectives: 23.9 us -> none
    dot_general x8 -> x0, matrix products: 21 us -> none  [one_block(): jnp.dot(window_piece, band_ones, preferred_element_type=jnp.float32)]
    concatenate x1 -> x0, local copies, waits for them, and re-layouts: 19.2 us -> none  [stacked(): jnp.concatenate([cross_terms, y_values, w_values[None, :], x_values[None,...]
    dynamic_slice x10 -> x0, local copies, waits for them, and re-layouts: 9.37 us -> none  [the longest x2 4.71 us: take_rows(): return lax.dynamic_slice_in_dim(padded, first + quota, length, 1)]
    all_gather x1 -> x0, blocking collectives: 8.07 us -> none  [stacked_from(): parts = lax.all_gather(parts, axes[k], axis=0, tiled=True)]
    convert_element_type x6 -> x0, other arithmetic: 8.06 us -> none  [the longest x1 5.16 us: per_device(): (returns.astype(jnp.float32) * weight[None, :]).astype(jnp.bfloat16)]
  transfers between devices with their start and end apart: 2 -> 0, of which waited for: 1 -> 0; matrix products, arithmetic and copies ran while one was open for 1% -> 0% of each run, Pallas kernels for 0% -> 0%
where the time goes in v1:
time: 56.9 us; the launch traced here: 56.6 us
  Pallas kernels  52.1 us (92%)
  local copies, waits for them, and re-layouts  2.22 us (4%)
  other arithmetic  1.62 us (3%)
  between operations  0.68 us (1%)
    pallas_call x1, Pallas kernels, exchange(): pl.pallas_call(functools.partial(exchange_kernel, groups, rows), out_shap...  44.1 us
    pallas_call x1, Pallas kernels, slopes(): pl.pallas_call(functools.partial(slope_kernel, rows), grid=(stocks // row...  8.07 us
    unnamed x2, local copies, waits for them, and re-layouts  2.18 us
    another operation x2, other arithmetic  1.53 us

profile of v1, /device:TPU:9, one launch (start us, length us, event | category | flops | bytes accessed | tf_op | source)
XLA Modules:
  0.0 56.6 jit_solution(10494669948359844116)
XLA Ops:
  0.7 0.8 %multiply_convert_fusion = bf16[8192]{0:T(1024)(128)(2,1)S(1)} fusion(s32[8192]{0:T(1024)} %param.6, bf16[8192]{0:T(1024)(128)(2,1)} %param.5), kind=kLoop, calls=%fused_computation.1 | loop fusion | flops 32768 | bytes 65536 | tf_op jit(solution)/shard_map/convert.3
  1.4 0.8 %convert_convert_fusion = bf16[8192]{0:T(1024)(128)(2,1)S(1)} fusion(s32[8192]{0:T(1024)} %param.6), kind=kLoop, calls=%fused_computation.2 | loop fusion | flops 16384 | bytes 49152 | tf_op jit(solution)/shard_map/convert.2
  2.2 0.1 pad_maximum_fusion.xw
  2.3 0.0 copy-start
  2.3 2.2 %copy-done = bf16[256,8192]{1,0:T(8,128)(2,1)S(1)} copy-done((bf16[256,8192]{1,0:T(8,128)(2,1)S(1)}, bf16[256,8192]{1,0:T(8,128)(2,1)}, u32[]{:S(2)}) %copy-start) | copy-done | bytes 4194328
  4.5 44.1 %exchange.1 = (bf16[256,5120]{1,0:T(8,128)(2,1)S(1)}, bf16[256,1024]{1,0:T(8,128)(2,1)S(1)}, bf16[2,5120]{1,0:T(2,128)(2,1)S(1)}, bf16[2,1024]{1,0:T(2,128)(2,1)S(1)}, s32[2,1,128]{2,1,0:T(1,128)S(1)}) custom-call(s32[1]{0:T(128)S(6)} %copy.5.counts, bf16[256,8192]{1,0:T(8,128)(2,1)S(1)} %copy-done, bf16[2,8192]{1,0:T(2,128)(2,1)S(1)} %pad_maximum_fusion.xw), custom_call_target="tpu_custom_call" | custom-call | tf_op jit(solution)/shard_map/exchange/pallas_call | solution.py:283
  48.6 8.1 %slopes.1 = f32[256,4096]{1,0:T(8,128)} custom-call(s32[2,1,128]{2,1,0:T(1,128)S(1)} %get-tuple-element.10.place, bf16[256,5120]{1,0:T(8,128)(2,1)S(1)} %get-tuple-element.11.near, bf16[256,1024]{1,0:T(8,128)(2,1)S(1)} %get-tuple-element.12.far, bf16[256,8192]{1,0:T(8,128)(2,1)S(1)} %copy-done, bf16[2,5120]{1,0:T(2,128)(2,1)S(1)} %get-tuple-element.13.nearx, ...), custom_call_target="tpu_custom_call" | custom-call | tf_op jit(solution)/shard_map/slopes/pallas_call | solution.py:361
  (2 shorter events, 0.0 us)
Async XLA Ops:
  2.3 2.2 %copy-start = (bf16[256,8192]{1,0:T(8,128)(2,1)S(1)}, bf16[256,8192]{1,0:T(8,128)(2,1)}, u32[]{:S(2)}) copy-start(bf16[256,8192]{1,0:T(8,128)(2,1)} %own.1) | copy-start | bytes 12582916

commit v2 on v1

v2 whole, which is shorter than its diff:
```python
import functools

import jax
import jax.numpy as jnp
from jax import lax
from jax.experimental import pallas as pl
from jax.experimental.pallas import tpu as pltpu
from jax.sharding import PartitionSpec as P

WIN = 1024
QROWS = 4096
CAP = 2 * QROWS
REACH = QROWS + WIN
RIDGE = 0.1
LANES = 128
TILE = 256
RT = REACH // LANES
OT = CAP // LANES
TT = WIN // LANES
MESH = pl.DeviceIdType.MESH
ZS, XS, YS = 8, 4, 4


def rolled(load, start, tiles, rows):
    first = lax.shift_right_logical(start, 7)
    r = jnp.bitwise_and(start, LANES - 1)
    turn = jnp.bitwise_and(LANES - r, LANES - 1)
    keep = lax.broadcasted_iota(jnp.int32, (rows, LANES), 1) < LANES - r
    turned = [pltpu.roll(load(first + j), turn, 1) for j in range(tiles + 1)]
    return [jnp.where(keep, turned[j], turned[j + 1]) for j in range(tiles)]


def moved_right(tiles, ticks, count):
    r = jnp.bitwise_and(ticks, LANES - 1)
    turned = [pltpu.roll(tile, r, 1) for tile in tiles]
    low = lax.broadcasted_iota(jnp.int32, tiles[0].shape, 1) < r
    n = len(tiles)
    at = {i: jnp.where(low, turned[max(i - 1, 0)], turned[min(i, n - 1)]) for i in range(n + 1)}
    for bit in (32, 16, 8, 4, 2, 1):
        taken = jnp.bitwise_and(ticks, bit * LANES) != 0
        moved = {}
        for i in range(count):
            if i in at and i - bit in at:
                moved[i] = jnp.where(taken, at[i - bit], at[i])
            elif i in at or i - bit in at:
                moved[i] = at[i] if i in at else at[i - bit]
        at = moved
    return at


def aligned(tiles, far_tiles, excess, edge):
    m = tiles.shape[1]
    parts = rolled(lambda k: tiles[jnp.minimum(jnp.maximum(k, 0), RT + OT - 1)], QROWS - excess, RT, m)
    older = rolled(lambda k: far_tiles[jnp.minimum(jnp.maximum(k, 0), TT - 1)], WIN - jnp.maximum(edge, 0), TT, m)
    lane = lax.broadcasted_iota(jnp.int32, (m, LANES), 1)
    for j in range(TT):
        parts[j] = jnp.where(lane < edge - j * LANES, older[j], parts[j])
    return jnp.concatenate(parts, 1)


def window_sums(a, pre, suf):
    m = a.shape[0]
    tiles, halo = REACH // TILE, WIN // TILE
    stack = jnp.concatenate([a[:, t * TILE : (t + 1) * TILE] for t in range(tiles)], 0)
    head = jnp.dot(stack, pre[...], preferred_element_type=jnp.float32)
    tail = jnp.dot(stack[: (tiles - halo) * m], suf[...], preferred_element_type=jnp.float32)
    whole = [head[t * m : (t + 1) * m, TILE - 1 :] for t in range(tiles)]
    result = []
    for t in range(halo, tiles):
        between = whole[t - 3] + whole[t - 2] + whole[t - 1]
        s = t - halo
        result.append(head[t * m : (t + 1) * m] + tail[s * m : (s + 1) * m] + between)
    return result


def span_kernel(sizes, counts, returns, market_in, mask_in, out, *scratch):
    groups = len(sizes)
    starts = [sum(sizes[:g]) for g in range(groups)]
    n = groups + 1
    it = iter(scratch)
    take = lambda k=n: [next(it) for _ in range(k)]
    ends, send, near, far, tiled, fars = take(), take(), take(), take(), take(), take()
    own = take(groups)
    pairin, zbuf, xbuf, ybuf, ebuf, place = take(6)
    pre, suf, stats, wx, market, mask = take(6)
    own_sem, near_ssem, cross_ssem, near_rsem, far_ssem, far_rsem, cnt_ssem, cnt_rsem = take(8)

    me = lax.axis_index("span")
    total = ZS * XS * YS * 2
    even = lax.rem(me, 2) == 0
    odd = lax.rem(me, 2) == 1
    last = me == total - 1
    chip = lax.div(me, 2)
    z = lax.rem(chip, ZS)
    x = lax.rem(lax.div(chip, ZS), XS)
    y = lax.div(chip, ZS * XS)

    def core0(yy, xx, zz):
        return ((yy * XS + xx) * ZS + zz) * 2

    def at_z(step):
        return core0(y, x, lax.rem(z + step + ZS, ZS))

    def at_x(step):
        return core0(y, lax.rem(x + step, XS), z)

    def at_y(step):
        return core0(lax.rem(y + step, YS), x, z)

    order = [groups] + list(range(groups))

    def remote(src, dst, ssem, rsem, target):
        return pltpu.make_async_remote_copy(
            src_ref=src, dst_ref=dst, send_sem=ssem, recv_sem=rsem, device_id=(target,), device_id_type=MESH
        )

    series = [
        pltpu.make_async_copy(market_in, market, own_sem.at[groups]),
        pltpu.make_async_copy(mask_in, mask, own_sem.at[n]),
    ]
    for load in series:
        load.start()
    loads = []
    for g in range(groups):
        load = pltpu.make_async_copy(returns.at[pl.ds(starts[g], sizes[g]), :], own[g], own_sem.at[g])
        load.start()
        loads.append(load)

    barrier = pltpu.get_barrier_semaphore()

    def hello(target):
        pl.semaphore_signal(barrier, inc=1, device_id=(target,), device_id_type=MESH)

    mine = counts[0]

    @pl.when(even)
    def _():
        hello(me + 1)

        @pl.when(me > 0)
        def _():
            hello(me - 1)

        for step in (1, 2, -1, -2):
            hello(at_z(step))
        for step in (1, 2, 3):
            hello(at_x(step))
            hello(at_y(step))

    @pl.when(odd)
    def _():
        hello(me - 1)

        @pl.when(jnp.logical_not(last))
        def _():
            hello(me + 1)

    pairin[...] = jnp.zeros_like(pairin) + mine

    @pl.when(me == 0)
    def _():
        for g in order:
            near[g][...] = jnp.zeros_like(near[g])

    def end_window(g):
        m = ends[g].shape[0]
        if g == groups:
            for load in series:
                load.wait()
            w = mask[...].astype(jnp.float32)
            v = market[...].astype(jnp.float32) * w
            for t in range(OT):
                tiled[g][RT + t] = jnp.concatenate([v[t : t + 1], w[t : t + 1]], 0).astype(jnp.bfloat16)
        else:
            loads[g].wait()
            for t in range(OT):
                tiled[g][RT + t] = own[g][:, t * LANES : (t + 1) * LANES]
        slot = lambda k: tiled[g][jnp.minimum(jnp.maximum(k, RT), RT + OT - 1)]
        for j, value in enumerate(rolled(slot, mine, RT, m)):
            ends[g][:, j * LANES : (j + 1) * LANES] = value

    def cross(g):
        @pl.when(odd)
        def _():
            remote(ends[g], near[g], near_ssem.at[g], near_rsem.at[g], me - 1).wait_recv()
            short = jnp.maximum(REACH - mine, 0)

            @pl.when(jnp.logical_not(last))
            def _():
                m = ends[g].shape[0]
                for first in range(0, m, 16):
                    part = min(m, 16)
                    b = slice(first, first + part)
                    tail = [near[g][b, QROWS + j * LANES : QROWS + (j + 1) * LANES] for j in range(TT)]
                    placed = moved_right(tail, short, RT + TT)
                    lane = lax.broadcasted_iota(jnp.int32, (part, LANES), 1)
                    for j in range(RT):
                        c = slice(j * LANES, (j + 1) * LANES)
                        send[g][b, c] = jnp.where(lane < short - j * LANES, placed[j + TT], ends[g][b, c])
                remote(send[g], near[g], cross_ssem.at[g], near_rsem.at[g], me + 1).start()

    def to_partner(g):
        @pl.when(even)
        def _():
            remote(ends[g], near[g], near_ssem.at[g], near_rsem.at[g], me + 1).start()

    end_window(order[0])
    end_window(order[1])

    @pl.when(even)
    def _():
        pl.semaphore_wait(barrier, 11 + jnp.where(me > 0, 1, 0))

    @pl.when(odd)
    def _():
        pl.semaphore_wait(barrier, 2 - jnp.where(last, 1, 0))
        remote(pairin, zbuf.at[0], cnt_ssem.at[0], cnt_rsem.at[0], me - 1).start()

    to_partner(order[0])
    to_partner(order[1])
    for i in range(2, n):
        end_window(order[i])
        to_partner(order[i])
        cross(order[i - 2])
    cross(order[n - 2])
    cross(order[n - 1])

    q = lax.broadcasted_iota(jnp.int32, (TILE, TILE), 0)
    p = lax.broadcasted_iota(jnp.int32, (TILE, TILE), 1)
    pre[...] = jnp.where(q <= p, 1.0, 0.0).astype(jnp.bfloat16)
    suf[...] = jnp.where(q > p, 1.0, 0.0).astype(jnp.bfloat16)

    @pl.when(even)
    def _():
        def arrival(dst, k):
            return remote(dst, dst, cnt_ssem.at[k], cnt_rsem.at[k], me + 1)

        sends = []

        def push(ref, target, k):
            copy = remote(ref, ref, cnt_ssem.at[k], cnt_rsem.at[k], target)
            copy.start()
            sends.append(copy)

        arrival(zbuf.at[0], 0).wait_recv()
        zbuf[z + 1] = zbuf[0] + mine
        for k, step in ((1, 1), (2, 2), (3, -1), (4, -2)):
            push(zbuf.at[z + 1], at_z(step), k)
        back1, back2 = lax.rem(z + ZS - 1, ZS), lax.rem(z + ZS - 2, ZS)
        ahead1, ahead2 = lax.rem(z + 1, ZS), lax.rem(z + 2, ZS)
        back3, back4, ahead3 = lax.rem(z + ZS - 3, ZS), lax.rem(z + ZS - 4, ZS), lax.rem(z + 3, ZS)
        for k, slot in ((1, back1), (2, back2), (3, ahead1), (4, ahead2)):
            arrival(zbuf.at[slot + 1], k).wait_recv()
        push(zbuf.at[back2 + 1], at_z(1), 5)
        push(zbuf.at[back2 + 1], at_z(2), 6)
        push(zbuf.at[ahead2 + 1], at_z(-1), 7)
        for k, slot in ((5, back3), (6, back4), (7, ahead3)):
            arrival(zbuf.at[slot + 1], k).wait_recv()
        column = zbuf[1]
        below = jnp.where(z > 0, zbuf[1], 0)
        for i in range(1, ZS):
            column = column + zbuf[i + 1]
            below = below + jnp.where(z > i, zbuf[i + 1], 0)
        xbuf[x] = column
        for step in (1, 2, 3):
            push(xbuf.at[x], at_x(step), 7 + step)
        for step in (1, 2, 3):
            arrival(xbuf.at[lax.rem(x + XS - step, XS)], 7 + step).wait_recv()
        plane = xbuf[0]
        below = below + jnp.where(x > 0, xbuf[0], 0)
        for i in range(1, XS):
            plane = plane + xbuf[i]
            below = below + jnp.where(x > i, xbuf[i], 0)
        ybuf[y] = plane
        for step in (1, 2, 3):
            push(ybuf.at[y], at_y(step), 10 + step)
        for step in (1, 2, 3):
            arrival(ybuf.at[lax.rem(y + YS - step, YS)], 10 + step).wait_recv()
        for i in range(YS):
            below = below + jnp.where(y > i, ybuf[i], 0)
        ebuf[0] = below - me * QROWS
        ebuf[1] = below + mine - (me + 1) * QROWS
        copy = remote(ebuf.at[pl.ds(0, 2)], ebuf.at[pl.ds(2, 2)], cnt_ssem.at[14], cnt_rsem.at[14], me + 1)
        copy.start()
        sends.append(copy)
        place[0] = ebuf[0]
        place[1] = jnp.full_like(ebuf[0], -1)
        for copy in sends:
            copy.wait_send()

    @pl.when(odd)
    def _():
        remote(ebuf.at[pl.ds(0, 2)], ebuf.at[pl.ds(2, 2)], cnt_ssem.at[14], cnt_rsem.at[14], me - 1).wait_recv()
        place[0] = ebuf[3]
        place[1] = ebuf[2] - (QROWS - WIN)

    excess = jnp.max(place[0])
    edge = jnp.max(place[1])
    for g in order:
        piece = near[g].at[:, pl.ds(QROWS, WIN)]

        @pl.when(even)
        def _():
            @pl.when(me > 0)
            def _():
                remote(send[g], near[g], cross_ssem.at[g], near_rsem.at[g], me + 1).wait_recv()

            remote(piece, far[g], far_ssem.at[g], far_rsem.at[g], me + 1).start()

        for t in range(RT):
            tiled[g][t] = near[g][:, t * LANES : (t + 1) * LANES]

        @pl.when(odd)
        def _():
            remote(piece, far[g], far_ssem.at[g], far_rsem.at[g], me - 1).wait_recv()
            for t in range(TT):
                fars[g][t] = far[g][:, t * LANES : (t + 1) * LANES]

        ticks = aligned(tiled[g], fars[g], excess, edge)
        if g == groups:
            wx[...] = ticks
            xf = ticks[0:1, :].astype(jnp.float32)
            wf = ticks[1:2, :].astype(jnp.float32)
            row = lax.broadcasted_iota(jnp.int32, (16, REACH), 0)
            a = jnp.where(row == 0, wf, jnp.where(row == 1, xf, xf * xf)).astype(jnp.bfloat16)
            for i, s in enumerate(window_sums(a, pre, suf)):
                c = slice(i * TILE, (i + 1) * TILE)
                sw, sx, sxx = s[0:1], s[1:2], s[2:3]
                stats[0:1, c] = sw
                stats[1:2, c] = sx
                stats[2:3, c] = 1.0 / (sw * sxx - sx * sx + RIDGE * WIN * WIN)
        else:
            m = sizes[g]
            yv = ticks * wx[1:2, :]
            crossed = (wx[0:1, :].astype(jnp.float32) * yv.astype(jnp.float32)).astype(jnp.bfloat16)
            for i, s in enumerate(window_sums(jnp.concatenate([crossed, yv], 0), pre, suf)):
                c = slice(i * TILE, (i + 1) * TILE)
                value = (stats[0:1, c] * s[:m] - stats[1:2, c] * s[m:]) * stats[2:3, c]
                out[starts[g] : starts[g] + m, c] = value

    @pl.when(even)
    def _():
        for g in order:
            remote(ends[g], near[g], near_ssem.at[g], near_rsem.at[g], me + 1).wait_send()
            remote(near[g].at[:, pl.ds(QROWS, WIN)], far[g], far_ssem.at[g], far_rsem.at[g], me + 1).wait_send()

    @pl.when(odd)
    def _():
        remote(pairin, zbuf.at[0], cnt_ssem.at[0], cnt_rsem.at[0], me - 1).wait_send()

        @pl.when(jnp.logical_not(last))
        def _():
            for g in order:
                remote(send[g], near[g], cross_ssem.at[g], near_rsem.at[g], me + 1).wait_send()


def slopes(counts, returns, market, mask, sizes):
    stocks = returns.shape[0]
    bf = jnp.bfloat16

    def per(shape):
        return [pltpu.VMEM(shape(m), bf) for m in list(sizes) + [2]]

    flat = lambda length: per(lambda m: (m, length))
    split = lambda count: per(lambda m: (count, m, LANES))
    n = len(sizes) + 1
    dma = pltpu.SemaphoreType.DMA
    row = lambda k: pltpu.VMEM((k, 1, LANES), jnp.int32)
    vmem = pl.BlockSpec(memory_space=pltpu.VMEM)
    return pl.pallas_call(
        functools.partial(span_kernel, sizes),
        out_shape=jax.ShapeDtypeStruct((stocks, QROWS), jnp.float32),
        in_specs=[pl.BlockSpec(memory_space=pltpu.SMEM)] + [pl.BlockSpec(memory_space=pltpu.HBM)] * 3,
        out_specs=vmem,
        scratch_shapes=flat(REACH) + flat(REACH) + flat(REACH) + flat(WIN) + split(RT + OT) + split(TT)
        + flat(CAP)[:-1]
        + [pltpu.VMEM((1, LANES), jnp.int32), row(ZS + 1), row(XS), row(YS), row(4), row(2)]
        + [pltpu.VMEM((TILE, TILE), bf)] * 2
        + [pltpu.VMEM((8, QROWS), jnp.float32), pltpu.VMEM((2, REACH), bf)]
        + [pltpu.VMEM((OT, LANES), bf), pltpu.VMEM((OT, LANES), jnp.int32)]
        + [dma((n + 1,))] * 6 + [dma((15,))] * 2,
        compiler_params=pltpu.CompilerParams(collective_id=0, has_side_effects=True, vmem_limit_bytes=48 << 20),
        name="slopes",
    )(counts, returns, market, mask)


def per_device(returns, market, mask, counts):
    sizes = (32,) * 8
    return slopes(counts, returns, market.reshape(OT, LANES), mask.reshape(OT, LANES), sizes)


def solution(mesh):
    return jax.shard_map(
        per_device,
        mesh=mesh,
        in_specs=(P(None, "span"), P("span"), P("span"), P("span")),
        out_specs=P(None, "span"),
        check_vma=False,
    )
```

time: 56.9 us -> 49.5 us (0.87)
  Pallas kernels: 52.1 us -> 45.2 us
  other arithmetic: 1.62 us -> 0 us
  local copies, waits for them, and re-layouts: 2.22 us -> 3.48 us
    pallas_call x2 -> x1, Pallas kernels: 52.1 us -> 45.2 us  [slopes(): pl.pallas_call(functools.partial(span_kernel, sizes), out_shape=jax.Shape...]
    another operation x3 -> x0, other arithmetic: 1.62 us -> none
    unnamed x2 -> x5, local copies, waits for them, and re-layouts: 2.18 us -> 3.48 us
where the time goes in v2:
time: 49.5 us; the launch traced here: 49.3 us
  Pallas kernels  45.2 us (91%)
  local copies, waits for them, and re-layouts  3.48 us (7%)
  between operations  0.67 us (1%)
    pallas_call x1, Pallas kernels, slopes(): pl.pallas_call(functools.partial(span_kernel, sizes), out_shape=jax.Shape...  45.2 us
    unnamed x5, local copies, waits for them, and re-layouts  3.48 us

profile of v2, /device:TPU:9, one launch (start us, length us, event | category | flops | bytes accessed | tf_op | source)
XLA Modules:
  0.0 49.3 jit_solution(16535000195525814585)
XLA Ops:
  0.7 0.0 copy-start
  0.7 0.7 %copy-done = s32[8192]{0:T(1024)S(1)} copy-done((s32[8192]{0:T(1024)S(1)}, s32[8192]{0:T(1024)}, u32[]{:S(2)}) %copy-start) | copy-done | bytes 32792
  1.4 0.0 copy-start.1
  1.4 0.7 %copy-done.1 = bf16[8192]{0:T(1024)(128)(2,1)S(1)} copy-done((bf16[8192]{0:T(1024)(128)(2,1)S(1)}, bf16[8192]{0:T(1024)(128)(2,1)}, u32[]{:S(2)}) %copy-start.1) | copy-done | bytes 16408
  2.1 45.2 %slopes.1 = f32[256,4096]{1,0:T(8,128)S(1)} custom-call(s32[1]{0:T(128)S(6)} %copy.6.counts, bf16[256,8192]{1,0:T(8,128)(2,1)} %returns.1, bf16[64,128]{1,0:T(8,128)(2,1)S(1)} %bitcast.3, s32[64,128]{1,0:T(8,128)S(1)} %bitcast.2), custom_call_target="tpu_custom_call" | custom-call | tf_op jit(solution)/shard_map/slopes/pallas_call | solution.py:370
  47.3 2.0 %copy.7 = f32[256,4096]{1,0:T(8,128)} copy(f32[256,4096]{1,0:T(8,128)S(1)} %slopes.1) | data formatting | bytes 8388608
Async XLA Ops:
  0.7 0.8 %copy-start = (s32[8192]{0:T(1024)S(1)}, s32[8192]{0:T(1024)}, u32[]{:S(2)}) copy-start(s32[8192]{0:T(1024)} %param.6) | copy-start | bytes 98308
  1.4 0.7 %copy-start.1 = (bf16[8192]{0:T(1024)(128)(2,1)S(1)}, bf16[8192]{0:T(1024)(128)(2,1)}, u32[]{:S(2)}) copy-start(bf16[8192]{0:T(1024)(128)(2,1)} %param.5) | copy-start | bytes 49156

commit v3 on v2

--- a/solution.py
+++ b/solution.py
@@ -83,7 +83,7 @@
     own = take(groups)
     pairin, zbuf, xbuf, ybuf, ebuf, place = take(6)
     pre, suf, stats, wx, market, mask = take(6)
-    own_sem, near_ssem, cross_ssem, near_rsem, far_ssem, far_rsem, cnt_ssem, cnt_rsem = take(8)
+    own_sem, near_ssem, cross_ssem, near_rsem, far_ssem, far_rsem, cnt_ssem, cnt_rsem, present = take(9)
 
     me = lax.axis_index("span")
     total = ZS * XS * YS * 2
@@ -146,14 +146,6 @@
         for step in (1, 2, 3):
             hello(at_x(step))
             hello(at_y(step))
-
-    @pl.when(odd)
-    def _():
-        hello(me - 1)
-
-        @pl.when(jnp.logical_not(last))
-        def _():
-            hello(me + 1)
 
     pairin[...] = jnp.zeros_like(pairin) + mine
 
@@ -207,14 +199,15 @@
     end_window(order[0])
     end_window(order[1])
 
+    @pl.when(odd)
+    def _():
+        pl.semaphore_wait(barrier, 2 - jnp.where(last, 1, 0))
+        pl.semaphore_signal(present, inc=1, device_id=(me - 1,), device_id_type=MESH)
+        remote(pairin, zbuf.at[0], cnt_ssem.at[0], cnt_rsem.at[0], me - 1).start()
+
     @pl.when(even)
     def _():
-        pl.semaphore_wait(barrier, 11 + jnp.where(me > 0, 1, 0))
-
-    @pl.when(odd)
-    def _():
-        pl.semaphore_wait(barrier, 2 - jnp.where(last, 1, 0))
-        remote(pairin, zbuf.at[0], cnt_ssem.at[0], cnt_rsem.at[0], me - 1).start()
+        pl.semaphore_wait(present, 1)
 
     to_partner(order[0])
     to_partner(order[1])
@@ -242,6 +235,7 @@
             copy.start()
             sends.append(copy)
 
+        pl.semaphore_wait(barrier, 10)
         arrival(zbuf.at[0], 0).wait_recv()
         zbuf[z + 1] = zbuf[0] + mine
         for k, step in ((1, 1), (2, 2), (3, -1), (4, -2)):
@@ -378,15 +372,16 @@
         + [pltpu.VMEM((TILE, TILE), bf)] * 2
         + [pltpu.VMEM((8, QROWS), jnp.float32), pltpu.VMEM((2, REACH), bf)]
         + [pltpu.VMEM((OT, LANES), bf), pltpu.VMEM((OT, LANES), jnp.int32)]
-        + [dma((n + 1,))] * 6 + [dma((15,))] * 2,
+        + [dma((n + 1,))] * 6 + [dma((15,))] * 2 + [pltpu.SemaphoreType.REGULAR],
         compiler_params=pltpu.CompilerParams(collective_id=0, has_side_effects=True, vmem_limit_bytes=48 << 20),
         name="slopes",
     )(counts, returns, market, mask)
 
 
 def per_device(returns, market, mask, counts):
-    sizes = (32,) * 8
-    return slopes(counts, returns, market.reshape(OT, LANES), mask.reshape(OT, LANES), sizes)
+    sizes = (16, 16, 32, 32, 32, 32, 32, 32, 16, 16)
+    far = lambda a: pltpu.with_memory_space_constraint(a, pltpu.HBM)
+    return slopes(counts, returns, far(market.reshape(OT, LANES)), far(mask.reshape(OT, LANES)), sizes)
 
 
 def solution(mesh):

time: 49.5 us -> 45.9 us (0.927)
  Pallas kernels: 45.2 us -> 42.7 us
  local copies, waits for them, and re-layouts: 3.48 us -> 2.02 us
    pallas_call x1, Pallas kernels: 45.2 us -> 42.7 us  [slopes(): pl.pallas_call(functools.partial(span_kernel, sizes), out_shape=jax.Shape...]
    unnamed x5 -> x1, local copies, waits for them, and re-layouts: 3.48 us -> 2.02 us
where the time goes in v3:
time: 45.9 us; the launch traced here: 45.4 us
  Pallas kernels  42.7 us (93%)
  local copies, waits for them, and re-layouts  2.02 us (4%)
  between operations  0.66 us (1%)
    pallas_call x1, Pallas kernels, slopes(): pl.pallas_call(functools.partial(span_kernel, sizes), out_shape=jax.Shape...  42.7 us
    unnamed x1, local copies, waits for them, and re-layouts  2.02 us

profile of v3, /device:TPU:9, one launch (start us, length us, event | category | flops | bytes accessed | tf_op | source)
XLA Modules:
  0.0 45.4 jit_solution(12404009446772756560)
XLA Ops:
  0.7 42.7 %slopes.1 = f32[256,4096]{1,0:T(8,128)S(1)} custom-call(s32[1]{0:T(128)S(6)} %copy.6.counts, bf16[256,8192]{1,0:T(8,128)(2,1)} %returns.1, bf16[64,128]{1,0:T(8,128)(2,1)} %bitcast.3, s32[64,128]{1,0:T(8,128)} %bitcast.2), custom_call_target="tpu_custom_call" | custom-call | tf_op jit(solution)/shard_map/slopes/pallas_call | solution.py:364
  43.4 2.0 %copy.7 = f32[256,4096]{1,0:T(8,128)} copy(f32[256,4096]{1,0:T(8,128)S(1)} %slopes.1) | data formatting | bytes 8388608

commit v4 on v3

--- a/solution.py
+++ b/solution.py
@@ -83,7 +83,7 @@
     own = take(groups)
     pairin, zbuf, xbuf, ybuf, ebuf, place = take(6)
     pre, suf, stats, wx, market, mask = take(6)
-    own_sem, near_ssem, cross_ssem, near_rsem, far_ssem, far_rsem, cnt_ssem, cnt_rsem, present = take(9)
+    own_sem, near_ssem, cross_ssem, near_rsem, far_ssem, far_rsem, cnt_ssem, cnt_rsem, present, ready = take(10)
 
     me = lax.axis_index("span")
     total = ZS * XS * YS * 2
@@ -145,7 +145,10 @@
             hello(at_z(step))
         for step in (1, 2, 3):
             hello(at_x(step))
-            hello(at_y(step))
+
+            @pl.when(y + step < YS)
+            def _(step=step):
+                hello(at_y(step))
 
     pairin[...] = jnp.zeros_like(pairin) + mine
 
@@ -235,7 +238,12 @@
             copy.start()
             sends.append(copy)
 
-        pl.semaphore_wait(barrier, 10)
+        pl.semaphore_wait(barrier, 7 + y)
+        for step in (1, 2, 3):
+            @pl.when(y >= step)
+            def _(step=step):
+                pl.semaphore_signal(ready, inc=1, device_id=(core0(y - step, x, z),), device_id_type=MESH)
+
         arrival(zbuf.at[0], 0).wait_recv()
         zbuf[z + 1] = zbuf[0] + mine
         for k, step in ((1, 1), (2, 2), (3, -1), (4, -2)):
@@ -266,10 +274,17 @@
             plane = plane + xbuf[i]
             below = below + jnp.where(x > i, xbuf[i], 0)
         ybuf[y] = plane
-        for step in (1, 2, 3):
-            push(ybuf.at[y], at_y(step), 10 + step)
-        for step in (1, 2, 3):
-            arrival(ybuf.at[lax.rem(y + YS - step, YS)], 10 + step).wait_recv()
+        @pl.when(y < YS - 1)
+        def _():
+            pl.semaphore_wait(ready, YS - 1 - y)
+
+        for step in (1, 2, 3):
+            up = remote(ybuf.at[y], ybuf.at[y], cnt_ssem.at[10 + step], cnt_rsem.at[10 + step], at_y(step))
+            pl.when(y + step < YS)(up.start)
+        for step in (1, 2, 3):
+            @pl.when(y >= step)
+            def _(step=step):
+                arrival(ybuf.at[y - step], 10 + step).wait_recv()
         for i in range(YS):
             below = below + jnp.where(y > i, ybuf[i], 0)
         ebuf[0] = below - me * QROWS
@@ -281,6 +296,9 @@
         place[1] = jnp.full_like(ebuf[0], -1)
         for copy in sends:
             copy.wait_send()
+        for step in (1, 2, 3):
+            up = remote(ybuf.at[y], ybuf.at[y], cnt_ssem.at[10 + step], cnt_rsem.at[10 + step], at_y(step))
+            pl.when(y + step < YS)(up.wait_send)
 
     @pl.when(odd)
     def _():
@@ -372,7 +390,7 @@
         + [pltpu.VMEM((TILE, TILE), bf)] * 2
         + [pltpu.VMEM((8, QROWS), jnp.float32), pltpu.VMEM((2, REACH), bf)]
         + [pltpu.VMEM((OT, LANES), bf), pltpu.VMEM((OT, LANES), jnp.int32)]
-        + [dma((n + 1,))] * 6 + [dma((15,))] * 2 + [pltpu.SemaphoreType.REGULAR],
+        + [dma((n + 1,))] * 6 + [dma((15,))] * 2 + [pltpu.SemaphoreType.REGULAR] * 2,
         compiler_params=pltpu.CompilerParams(collective_id=0, has_side_effects=True, vmem_limit_bytes=48 << 20),
         name="slopes",
     )(counts, returns, market, mask)

time: 45.9 us -> 45.9 us (level)
  no operation moved by 1% of the time
where the time goes in v4:
time: 45.9 us; the launch traced here: 45.4 us
  Pallas kernels  42.7 us (93%)
  local copies, waits for them, and re-layouts  2.02 us (4%)
  between operations  0.66 us (1%)
    pallas_call x1, Pallas kernels, slopes(): pl.pallas_call(functools.partial(span_kernel, sizes), out_shape=jax.Shape...  42.7 us
    unnamed x1, local copies, waits for them, and re-layouts  2.02 us

profile of v4, /device:TPU:9, one launch (start us, length us, event | category | flops | bytes accessed | tf_op | source)
XLA Modules:
  0.0 45.4 jit_solution(7777152482544102690)
XLA Ops:
  0.7 42.7 %slopes.1 = f32[256,4096]{1,0:T(8,128)S(1)} custom-call(s32[1]{0:T(128)S(6)} %copy.6.counts, bf16[256,8192]{1,0:T(8,128)(2,1)} %returns.1, bf16[64,128]{1,0:T(8,128)(2,1)} %bitcast.3, s32[64,128]{1,0:T(8,128)} %bitcast.2), custom_call_target="tpu_custom_call" | custom-call | tf_op jit(solution)/shard_map/slopes/pallas_call | solution.py:382
  43.4 2.0 %copy.7 = f32[256,4096]{1,0:T(8,128)} copy(f32[256,4096]{1,0:T(8,128)S(1)} %slopes.1) | data formatting | bytes 8388608

commit v5 on v4

--- a/solution.py
+++ b/solution.py
@@ -83,7 +83,8 @@
     own = take(groups)
     pairin, zbuf, xbuf, ybuf, ebuf, place = take(6)
     pre, suf, stats, wx, market, mask = take(6)
-    own_sem, near_ssem, cross_ssem, near_rsem, far_ssem, far_rsem, cnt_ssem, cnt_rsem, present, ready = take(10)
+    own_sem, near_ssem, cross_ssem, near_rsem, far_ssem, far_rsem, cnt_ssem, cnt_rsem, leg_ssem, leg_rsem, present, ready = take(12)
+    legs = take(2)
 
     me = lax.axis_index("span")
     total = ZS * XS * YS * 2
@@ -95,6 +96,8 @@
     x = lax.rem(lax.div(chip, ZS), XS)
     y = lax.div(chip, ZS * XS)
 
+    odd_core = lax.rem(me, 2) == 1
+
     def core0(yy, xx, zz):
         return ((yy * XS + xx) * ZS + zz) * 2
 
@@ -107,7 +110,12 @@
     def at_y(step):
         return core0(lax.rem(y + step, YS), x, z)
 
-    order = [groups] + list(range(groups))
+    around = [k for k in range(groups) if sizes[k] == 32][-2:]
+    rest = [k for k in range(1, groups) if k not in around]
+    order = [0, groups] + around + rest
+    done = [groups, 0] + rest[:-2] + around + rest[-2:]
+    inner = lax.div(me, 2 * ZS) < XS * YS - 1
+    leg = jnp.logical_and(odd_core, jnp.logical_and(inner, jnp.logical_or(z == 1, z == 4)))
 
     def remote(src, dst, ssem, rsem, target):
         return pltpu.make_async_remote_copy(
@@ -118,13 +126,12 @@
         pltpu.make_async_copy(market_in, market, own_sem.at[groups]),
         pltpu.make_async_copy(mask_in, mask, own_sem.at[n]),
     ]
+    loads = [
+        pltpu.make_async_copy(returns.at[pl.ds(starts[g], sizes[g]), :], own[g], own_sem.at[g]) for g in range(groups)
+    ]
+    loads[0].start()
     for load in series:
         load.start()
-    loads = []
-    for g in range(groups):
-        load = pltpu.make_async_copy(returns.at[pl.ds(starts[g], sizes[g]), :], own[g], own_sem.at[g])
-        load.start()
-        loads.append(load)
 
     barrier = pltpu.get_barrier_semaphore()
 
@@ -149,6 +156,14 @@
             @pl.when(y + step < YS)
             def _(step=step):
                 hello(at_y(step))
+
+    @pl.when(jnp.logical_and(even, jnp.logical_and(z == 0, me > 0)))
+    def _():
+        hello(me - 13)
+
+    @pl.when(leg)
+    def _():
+        hello(me + 6)
 
     pairin[...] = jnp.zeros_like(pairin) + mine
 
@@ -192,7 +207,18 @@
                     for j in range(RT):
                         c = slice(j * LANES, (j + 1) * LANES)
                         send[g][b, c] = jnp.where(lane < short - j * LANES, placed[j + TT], ends[g][b, c])
-                remote(send[g], near[g], cross_ssem.at[g], near_rsem.at[g], me + 1).start()
+                if g in around:
+                    k = around.index(g)
+
+                    @pl.when(z == ZS - 1)
+                    def _():
+                        remote(send[g], legs[k], cross_ssem.at[g], leg_rsem.at[k], me - 6).start()
+
+                    @pl.when(z < ZS - 1)
+                    def _():
+                        remote(send[g], near[g], cross_ssem.at[g], near_rsem.at[g], me + 1).start()
+                else:
+                    remote(send[g], near[g], cross_ssem.at[g], near_rsem.at[g], me + 1).start()
 
     def to_partner(g):
         @pl.when(even)
@@ -200,11 +226,14 @@
             remote(ends[g], near[g], near_ssem.at[g], near_rsem.at[g], me + 1).start()
 
     end_window(order[0])
+    for g in order[2:]:
+        loads[g].start()
     end_window(order[1])
 
     @pl.when(odd)
     def _():
-        pl.semaphore_wait(barrier, 2 - jnp.where(last, 1, 0))
+        more = jnp.logical_and(inner, jnp.logical_or(jnp.logical_or(z == 1, z == 4), z == 7))
+        pl.semaphore_wait(barrier, 2 - jnp.where(last, 1, 0) + jnp.where(more, 1, 0))
         pl.semaphore_signal(present, inc=1, device_id=(me - 1,), device_id_type=MESH)
         remote(pairin, zbuf.at[0], cnt_ssem.at[0], cnt_rsem.at[0], me - 1).start()
 
@@ -220,6 +249,21 @@
         cross(order[i - 2])
     cross(order[n - 2])
     cross(order[n - 1])
+
+    def onward(k, start):
+        @pl.when(z == 4)
+        def _():
+            start(remote(legs[k], legs[k], leg_ssem.at[k], leg_rsem.at[k], me - 6))
+
+        @pl.when(z == 1)
+        def _():
+            start(remote(legs[k], near[around[k]], leg_ssem.at[k], near_rsem.at[around[k]], me + 13))
+
+    @pl.when(leg)
+    def _():
+        for k in range(len(around)):
+            remote(legs[k], legs[k], leg_ssem.at[k], leg_rsem.at[k], me + 6).wait_recv()
+            onward(k, lambda copy: copy.start())
 
     q = lax.broadcasted_iota(jnp.int32, (TILE, TILE), 0)
     p = lax.broadcasted_iota(jnp.int32, (TILE, TILE), 1)
@@ -308,7 +352,7 @@
 
     excess = jnp.max(place[0])
     edge = jnp.max(place[1])
-    for g in order:
+    for g in done:
         piece = near[g].at[:, pl.ds(QROWS, WIN)]
 
         @pl.when(even)
@@ -365,6 +409,11 @@
             for g in order:
                 remote(send[g], near[g], cross_ssem.at[g], near_rsem.at[g], me + 1).wait_send()
 
+        @pl.when(leg)
+        def _():
+            for k in range(len(around)):
+                onward(k, lambda copy: copy.wait_send())
+
 
 def slopes(counts, returns, market, mask, sizes):
     stocks = returns.shape[0]
@@ -390,7 +439,8 @@
         + [pltpu.VMEM((TILE, TILE), bf)] * 2
         + [pltpu.VMEM((8, QROWS), jnp.float32), pltpu.VMEM((2, REACH), bf)]
         + [pltpu.VMEM((OT, LANES), bf), pltpu.VMEM((OT, LANES), jnp.int32)]
-        + [dma((n + 1,))] * 6 + [dma((15,))] * 2 + [pltpu.SemaphoreType.REGULAR] * 2,
+        + [dma((n + 1,))] * 6 + [dma((15,))] * 2 + [dma((2,))] * 2 + [pltpu.SemaphoreType.REGULAR] * 2
+        + [pltpu.VMEM((32, REACH), bf)] * 2,
         compiler_params=pltpu.CompilerParams(collective_id=0, has_side_effects=True, vmem_limit_bytes=48 << 20),
         name="slopes",
     )(counts, returns, market, mask)

time: 45.9 us -> 47.7 us (1.039)
  Pallas kernels: 42.7 us -> 44.7 us
    pallas_call x1, Pallas kernels: 42.7 us -> 44.7 us  [slopes(): pl.pallas_call(functools.partial(span_kernel, sizes), out_shape=jax.Shape...]
where the time goes in v5:
time: 47.7 us; the launch traced here: 47.3 us
  Pallas kernels  44.7 us (94%)
  local copies, waits for them, and re-layouts  2.02 us (4%)
  between operations  0.66 us (1%)
    pallas_call x1, Pallas kernels, slopes(): pl.pallas_call(functools.partial(span_kernel, sizes), out_shape=jax.Shape...  44.7 us
    unnamed x1, local copies, waits for them, and re-layouts  2.02 us

profile of v5, /device:TPU:9, one launch (start us, length us, event | category | flops | bytes accessed | tf_op | source)
XLA Modules:
  0.0 47.3 jit_solution(2621018063628275956)
XLA Ops:
  0.7 44.7 %slopes.1 = f32[256,4096]{1,0:T(8,128)S(1)} custom-call(s32[1]{0:T(128)S(6)} %copy.6.counts, bf16[256,8192]{1,0:T(8,128)(2,1)} %returns.1, bf16[64,128]{1,0:T(8,128)(2,1)} %bitcast.3, s32[64,128]{1,0:T(8,128)} %bitcast.2), custom_call_target="tpu_custom_call" | custom-call | tf_op jit(solution)/shard_map/slopes/pallas_call | solution.py:431
  45.3 2.0 %copy.7 = f32[256,4096]{1,0:T(8,128)} copy(f32[256,4096]{1,0:T(8,128)S(1)} %slopes.1) | data formatting | bytes 8388608

commit v6 on v5

--- a/solution.py
+++ b/solution.py
@@ -110,12 +110,15 @@
     def at_y(step):
         return core0(lax.rem(y + step, YS), x, z)
 
-    around = [k for k in range(groups) if sizes[k] == 32][-2:]
+    around = [7, 1]
     rest = [k for k in range(1, groups) if k not in around]
     order = [0, groups] + around + rest
     done = [groups, 0] + rest[:-2] + around + rest[-2:]
-    inner = lax.div(me, 2 * ZS) < XS * YS - 1
-    leg = jnp.logical_and(odd_core, jnp.logical_and(inner, jnp.logical_or(z == 1, z == 4)))
+    column = lax.div(me, 2 * ZS)
+    inner = column < XS * YS - 1
+    leg_a = jnp.logical_and(odd_core, jnp.logical_and(inner, z == 4))
+    leg_b = jnp.logical_and(odd_core, jnp.logical_and(column > 0, z == 1))
+    first_leg = jnp.logical_and(odd_core, jnp.logical_and(inner, z == 7))
 
     def remote(src, dst, ssem, rsem, target):
         return pltpu.make_async_remote_copy(
@@ -159,9 +162,13 @@
 
     @pl.when(jnp.logical_and(even, jnp.logical_and(z == 0, me > 0)))
     def _():
-        hello(me - 13)
-
-    @pl.when(leg)
+        hello(me + 3)
+
+    @pl.when(leg_b)
+    def _():
+        hello(me - 10)
+
+    @pl.when(leg_a)
     def _():
         hello(me + 6)
 
@@ -225,14 +232,13 @@
         def _():
             remote(ends[g], near[g], near_ssem.at[g], near_rsem.at[g], me + 1).start()
 
-    end_window(order[0])
     for g in order[2:]:
         loads[g].start()
-    end_window(order[1])
+    end_window(order[0])
 
     @pl.when(odd)
     def _():
-        more = jnp.logical_and(inner, jnp.logical_or(jnp.logical_or(z == 1, z == 4), z == 7))
+        more = jnp.logical_or(jnp.logical_or(leg_a, leg_b), first_leg)
         pl.semaphore_wait(barrier, 2 - jnp.where(last, 1, 0) + jnp.where(more, 1, 0))
         pl.semaphore_signal(present, inc=1, device_id=(me - 1,), device_id_type=MESH)
         remote(pairin, zbuf.at[0], cnt_ssem.at[0], cnt_rsem.at[0], me - 1).start()
@@ -242,28 +248,27 @@
         pl.semaphore_wait(present, 1)
 
     to_partner(order[0])
+    end_window(order[1])
     to_partner(order[1])
+    cross(order[0])
     for i in range(2, n):
         end_window(order[i])
         to_partner(order[i])
-        cross(order[i - 2])
-    cross(order[n - 2])
+        cross(order[i - 1])
     cross(order[n - 1])
 
-    def onward(k, start):
-        @pl.when(z == 4)
-        def _():
-            start(remote(legs[k], legs[k], leg_ssem.at[k], leg_rsem.at[k], me - 6))
-
-        @pl.when(z == 1)
-        def _():
-            start(remote(legs[k], near[around[k]], leg_ssem.at[k], near_rsem.at[around[k]], me + 13))
-
-    @pl.when(leg)
-    def _():
-        for k in range(len(around)):
-            remote(legs[k], legs[k], leg_ssem.at[k], leg_rsem.at[k], me + 6).wait_recv()
-            onward(k, lambda copy: copy.start())
+    def onward_a(k):
+        return remote(legs[k], legs[k], leg_ssem.at[k], leg_rsem.at[k], me + 10)
+
+    def onward_b(k):
+        return remote(legs[k], near[around[k]], leg_ssem.at[k], near_rsem.at[around[k]], me - 3)
+
+    for on, onward in ((leg_a, onward_a), (leg_b, onward_b)):
+        @pl.when(on)
+        def _(onward=onward):
+            for k in range(len(around)):
+                onward_a(k).wait_recv()
+                onward(k).start()
 
     q = lax.broadcasted_iota(jnp.int32, (TILE, TILE), 0)
     p = lax.broadcasted_iota(jnp.int32, (TILE, TILE), 1)
@@ -409,10 +414,11 @@
             for g in order:
                 remote(send[g], near[g], cross_ssem.at[g], near_rsem.at[g], me + 1).wait_send()
 
-        @pl.when(leg)
-        def _():
-            for k in range(len(around)):
-                onward(k, lambda copy: copy.wait_send())
+        for on, onward in ((leg_a, onward_a), (leg_b, onward_b)):
+            @pl.when(on)
+            def _(onward=onward):
+                for k in range(len(around)):
+                    onward(k).wait_send()
 
 
 def slopes(counts, returns, market, mask, sizes):
@@ -440,7 +446,7 @@
         + [pltpu.VMEM((8, QROWS), jnp.float32), pltpu.VMEM((2, REACH), bf)]
         + [pltpu.VMEM((OT, LANES), bf), pltpu.VMEM((OT, LANES), jnp.int32)]
         + [dma((n + 1,))] * 6 + [dma((15,))] * 2 + [dma((2,))] * 2 + [pltpu.SemaphoreType.REGULAR] * 2
-        + [pltpu.VMEM((32, REACH), bf)] * 2,
+        + [pltpu.VMEM((sizes[k], REACH), bf) for k in (7, 1)],
         compiler_params=pltpu.CompilerParams(collective_id=0, has_side_effects=True, vmem_limit_bytes=48 << 20),
         name="slopes",
     )(counts, returns, market, mask)

time: 47.7 us -> 41 us (0.86)
  Pallas kernels: 44.7 us -> 37.9 us
    pallas_call x1, Pallas kernels: 44.7 us -> 37.9 us  [slopes(): pl.pallas_call(functools.partial(span_kernel, sizes), out_shape=jax.Shape...]
where the time goes in v6:
time: 41 us; the launch traced here: 40.6 us
  Pallas kernels  37.9 us (92%)
  local copies, waits for them, and re-layouts  2.02 us (5%)
  between operations  0.66 us (2%)
    pallas_call x1, Pallas kernels, slopes(): pl.pallas_call(functools.partial(span_kernel, sizes), out_shape=jax.Shape...  37.9 us
    unnamed x1, local copies, waits for them, and re-layouts  2.02 us

profile of v6, /device:TPU:9, one launch (start us, length us, event | category | flops | bytes accessed | tf_op | source)
XLA Modules:
  0.0 40.6 jit_solution(6188511521455161498)
XLA Ops:
  0.7 37.9 %slopes.1 = f32[256,4096]{1,0:T(8,128)S(1)} custom-call(s32[1]{0:T(128)S(6)} %copy.6.counts, bf16[256,8192]{1,0:T(8,128)(2,1)} %returns.1, bf16[64,128]{1,0:T(8,128)(2,1)} %bitcast.3, s32[64,128]{1,0:T(8,128)} %bitcast.2), custom_call_target="tpu_custom_call" | custom-call | tf_op jit(solution)/shard_map/slopes/pallas_call | solution.py:437
  38.6 2.0 %copy.7 = f32[256,4096]{1,0:T(8,128)} copy(f32[256,4096]{1,0:T(8,128)S(1)} %slopes.1) | data formatting | bytes 8388608

commit v7 on v6

--- a/solution.py
+++ b/solution.py
@@ -110,7 +110,7 @@
     def at_y(step):
         return core0(lax.rem(y + step, YS), x, z)
 
-    around = [7, 1]
+    around = [7, 6]
     rest = [k for k in range(1, groups) if k not in around]
     order = [0, groups] + around + rest
     done = [groups, 0] + rest[:-2] + around + rest[-2:]
@@ -251,10 +251,16 @@
     end_window(order[1])
     to_partner(order[1])
     cross(order[0])
+    cross(order[1])
     for i in range(2, n):
         end_window(order[i])
         to_partner(order[i])
-        cross(order[i - 1])
+        if i == 2:
+            cross(order[i])
+        elif i == 3:
+            continue
+        else:
+            cross(order[i - 1])
     cross(order[n - 1])
 
     def onward_a(k):
@@ -446,7 +452,7 @@
         + [pltpu.VMEM((8, QROWS), jnp.float32), pltpu.VMEM((2, REACH), bf)]
         + [pltpu.VMEM((OT, LANES), bf), pltpu.VMEM((OT, LANES), jnp.int32)]
         + [dma((n + 1,))] * 6 + [dma((15,))] * 2 + [dma((2,))] * 2 + [pltpu.SemaphoreType.REGULAR] * 2
-        + [pltpu.VMEM((sizes[k], REACH), bf) for k in (7, 1)],
+        + [pltpu.VMEM((sizes[k], REACH), bf) for k in (7, 6)],
         compiler_params=pltpu.CompilerParams(collective_id=0, has_side_effects=True, vmem_limit_bytes=48 << 20),
         name="slopes",
     )(counts, returns, market, mask)

time: 41 us -> 39.9 us (0.973)
  Pallas kernels: 37.9 us -> 36.5 us
    pallas_call x1, Pallas kernels: 37.9 us -> 36.5 us  [slopes(): pl.pallas_call(functools.partial(span_kernel, sizes), out_shape=jax.Shape...]
where the time goes in v7:
time: 39.9 us; the launch traced here: 39.2 us
  Pallas kernels  36.5 us (91%)
  local copies, waits for them, and re-layouts  2.02 us (5%)
  between operations  0.66 us (2%)
    pallas_call x1, Pallas kernels, slopes(): pl.pallas_call(functools.partial(span_kernel, sizes), out_shape=jax.Shape...  36.5 us
    unnamed x1, local copies, waits for them, and re-layouts  2.02 us

profile of v7, /device:TPU:9, one launch (start us, length us, event | category | flops | bytes accessed | tf_op | source)
XLA Modules:
  0.0 39.2 jit_solution(4988705391539187704)
XLA Ops:
  0.7 36.5 %slopes.1 = f32[256,4096]{1,0:T(8,128)S(1)} custom-call(s32[1]{0:T(128)S(6)} %copy.6.counts, bf16[256,8192]{1,0:T(8,128)(2,1)} %returns.1, bf16[64,128]{1,0:T(8,128)(2,1)} %bitcast.3, s32[64,128]{1,0:T(8,128)} %bitcast.2), custom_call_target="tpu_custom_call" | custom-call | tf_op jit(solution)/shard_map/slopes/pallas_call | solution.py:443
  37.2 2.0 %copy.7 = f32[256,4096]{1,0:T(8,128)} copy(f32[256,4096]{1,0:T(8,128)S(1)} %slopes.1) | data formatting | bytes 8388608

commit v8 on v7

--- a/solution.py
+++ b/solution.py
@@ -84,7 +84,9 @@
     pairin, zbuf, xbuf, ybuf, ebuf, place = take(6)
     pre, suf, stats, wx, market, mask = take(6)
     own_sem, near_ssem, cross_ssem, near_rsem, far_ssem, far_rsem, cnt_ssem, cnt_rsem, leg_ssem, leg_rsem, present, ready = take(12)
+    step_ssem, step_rsem, okay = take(3)
     legs = take(2)
+    stepped = next(it)
 
     me = lax.axis_index("span")
     total = ZS * XS * YS * 2
@@ -113,11 +115,13 @@
     around = [7, 6]
     rest = [k for k in range(1, groups) if k not in around]
     order = [0, groups] + around + rest
-    done = [groups, 0] + rest[:-2] + around + rest[-2:]
+    done = [groups, 0] + rest[1:-2] + around + [1] + rest[-2:]
     column = lax.div(me, 2 * ZS)
     inner = column < XS * YS - 1
     leg_a = jnp.logical_and(odd_core, jnp.logical_and(inner, z == 4))
     leg_b = jnp.logical_and(odd_core, jnp.logical_and(column > 0, z == 1))
+    step_a = jnp.logical_and(odd_core, z == 0)
+    step_b = jnp.logical_and(odd_core, z == 5)
     first_leg = jnp.logical_and(odd_core, jnp.logical_and(inner, z == 7))
 
     def remote(src, dst, ssem, rsem, target):
@@ -163,6 +167,15 @@
     @pl.when(jnp.logical_and(even, jnp.logical_and(z == 0, me > 0)))
     def _():
         hello(me + 3)
+
+    @pl.when(jnp.logical_and(even, z == 4))
+    def _():
+        hello(me + 3)
+
+    @pl.when(step_a)
+    def _():
+        hello(me + 6)
+        hello(me + 10)
 
     @pl.when(leg_b)
     def _():
@@ -224,6 +237,14 @@
                     @pl.when(z < ZS - 1)
                     def _():
                         remote(send[g], near[g], cross_ssem.at[g], near_rsem.at[g], me + 1).start()
+                elif g == 1:
+                    @pl.when(z == 3)
+                    def _():
+                        remote(send[g], stepped, cross_ssem.at[g], step_rsem, me - 6).start()
+
+                    @pl.when(z != 3)
+                    def _():
+                        remote(send[g], near[g], cross_ssem.at[g], near_rsem.at[g], me + 1).start()
                 else:
                     remote(send[g], near[g], cross_ssem.at[g], near_rsem.at[g], me + 1).start()
 
@@ -238,8 +259,12 @@
 
     @pl.when(odd)
     def _():
-        more = jnp.logical_or(jnp.logical_or(leg_a, leg_b), first_leg)
-        pl.semaphore_wait(barrier, 2 - jnp.where(last, 1, 0) + jnp.where(more, 1, 0))
+        more = jnp.logical_or(jnp.logical_or(leg_a, leg_b), jnp.logical_or(first_leg, z == 3))
+        pl.semaphore_wait(barrier, 2 - jnp.where(last, 1, 0) + jnp.where(more, 1, 0) + jnp.where(z == 5, 2, 0))
+        @pl.when(z == 5)
+        def _():
+            pl.semaphore_signal(okay, inc=1, device_id=(me - 10,), device_id_type=MESH)
+
         pl.semaphore_signal(present, inc=1, device_id=(me - 1,), device_id_type=MESH)
         remote(pairin, zbuf.at[0], cnt_ssem.at[0], cnt_rsem.at[0], me - 1).start()
 
@@ -268,6 +293,20 @@
 
     def onward_b(k):
         return remote(legs[k], near[around[k]], leg_ssem.at[k], near_rsem.at[around[k]], me - 3)
+
+    onto_b = remote(stepped, stepped, step_ssem, step_rsem, me + 10)
+    onto_c = remote(stepped, near[1], step_ssem, near_rsem.at[1], me - 3)
+
+    @pl.when(step_a)
+    def _():
+        onto_b.wait_recv()
+        pl.semaphore_wait(okay, 1)
+        onto_b.start()
+
+    @pl.when(step_b)
+    def _():
+        onto_b.wait_recv()
+        onto_c.start()
 
     for on, onward in ((leg_a, onward_a), (leg_b, onward_b)):
         @pl.when(on)
@@ -426,6 +465,9 @@
                 for k in range(len(around)):
                     onward(k).wait_send()
 
+        pl.when(step_a)(onto_b.wait_send)
+        pl.when(step_b)(onto_c.wait_send)
+
 
 def slopes(counts, returns, market, mask, sizes):
     stocks = returns.shape[0]
@@ -451,8 +493,8 @@
         + [pltpu.VMEM((TILE, TILE), bf)] * 2
         + [pltpu.VMEM((8, QROWS), jnp.float32), pltpu.VMEM((2, REACH), bf)]
         + [pltpu.VMEM((OT, LANES), bf), pltpu.VMEM((OT, LANES), jnp.int32)]
-        + [dma((n + 1,))] * 6 + [dma((15,))] * 2 + [dma((2,))] * 2 + [pltpu.SemaphoreType.REGULAR] * 2
-        + [pltpu.VMEM((sizes[k], REACH), bf) for k in (7, 6)],
+        + [dma((n + 1,))] * 6 + [dma((15,))] * 2 + [dma((2,))] * 2 + [pltpu.SemaphoreType.REGULAR] * 2 + [dma] * 2 + [pltpu.SemaphoreType.REGULAR]
+        + [pltpu.VMEM((sizes[k], REACH), bf) for k in (7, 6)] + [pltpu.VMEM((sizes[1], REACH), bf)],
         compiler_params=pltpu.CompilerParams(collective_id=0, has_side_effects=True, vmem_limit_bytes=48 << 20),
         name="slopes",
     )(counts, returns, market, mask)

time: 39.9 us -> 41.6 us (1.043)
  Pallas kernels: 36.5 us -> 38.6 us
    pallas_call x1, Pallas kernels: 36.5 us -> 38.6 us  [slopes(): pl.pallas_call(functools.partial(span_kernel, sizes), out_shape=jax.Shape...]
where the time goes in v8:
time: 41.6 us; the launch traced here: 41.2 us
  Pallas kernels  38.6 us (93%)
  local copies, waits for them, and re-layouts  2.02 us (5%)
  between operations  0.66 us (2%)
    pallas_call x1, Pallas kernels, slopes(): pl.pallas_call(functools.partial(span_kernel, sizes), out_shape=jax.Shape...  38.6 us
    unnamed x1, local copies, waits for them, and re-layouts  2.02 us

profile of v8, /device:TPU:9, one launch (start us, length us, event | category | flops | bytes accessed | tf_op | source)
XLA Modules:
  0.0 41.2 jit_solution(18037019430784038220)
XLA Ops:
  0.7 38.6 %slopes.1 = f32[256,4096]{1,0:T(8,128)S(1)} custom-call(s32[1]{0:T(128)S(6)} %copy.6.counts, bf16[256,8192]{1,0:T(8,128)(2,1)} %returns.1, bf16[64,128]{1,0:T(8,128)(2,1)} %bitcast.3, s32[64,128]{1,0:T(8,128)} %bitcast.2), custom_call_target="tpu_custom_call" | custom-call | tf_op jit(solution)/shard_map/slopes/pallas_call | solution.py:485
  39.2 2.0 %copy.7 = f32[256,4096]{1,0:T(8,128)} copy(f32[256,4096]{1,0:T(8,128)S(1)} %slopes.1) | data formatting | bytes 8388608
